TPU v7x, 128 devices: a whole 4x4x4 slice. The times are simulated.
128 devices in a mesh: batch: 1, group: 128 (over z, y, x, core).
Axes of the slice: x: 4, y: 4, z: 4, core: 2. Of those that a mesh axis runs over, the one named last changes fastest.
Arguments:
- sort_keys: float32 [65536], P(('batch', 'group'))
- seg_ids: int32 [65536], P(('batch', 'group'))
- payload: bfloat16 [65536, 2048], P(('batch', 'group'))
Outputs:
- output: bfloat16 [65536, 2048], P(('batch', 'group'))
All inputs are finite; a program needn't handle non-finite values.
Results may differ from a plain program's by a relative error of at most 0.00688365.
Values are sent between devices in bfloat16 or wider.
A program may use at most 1 GiB of HBM per device.

v0:
```python
import jax
import jax.numpy as jnp
from jax import lax
from jax.sharding import PartitionSpec as P


def combine_runs(left_part, right_part):
    left_flag, left_rows = left_part
    right_flag, right_rows = right_part
    joined = jnp.where(right_flag[..., None], right_rows, left_rows + right_rows)
    return jnp.logical_or(left_flag, right_flag), joined


def solution(mesh):
    group_size = mesh.shape['group']

    def per_device(sort_keys, seg_ids, payload):
        rows_dev = sort_keys.shape[0]
        width = payload.shape[1]
        pair_rows = rows_dev // group_size
        capacity = 2 * pair_rows
        my_index = lax.axis_index('group')
        local_pos = jnp.arange(rows_dev, dtype=jnp.int32)
        sorted_keys, sorted_seg, local_order = lax.sort((sort_keys, seg_ids, local_pos), num_keys=1)
        samples = sorted_keys.reshape(group_size, pair_rows)[:, 0]
        all_samples = lax.all_gather(samples, 'group', tiled=True)
        ordered_samples = jnp.sort(all_samples)
        splitters = ordered_samples.reshape(group_size, group_size)[1:, group_size // 2]
        inner_starts = jnp.searchsorted(sorted_keys, splitters, side='left').astype(jnp.int32)
        bucket_start = jnp.concatenate([jnp.zeros((1,), jnp.int32), inner_starts])
        bucket_end = jnp.concatenate([inner_starts, jnp.full((1,), rows_dev, jnp.int32)])
        slot_ids = jnp.arange(capacity, dtype=jnp.int32)
        src_index = bucket_start[:, None] + slot_ids[None, :]
        in_bucket = src_index < bucket_end[:, None]
        src_clip = jnp.minimum(src_index, rows_dev - 1)
        send_keys = jnp.where(in_bucket, sorted_keys[src_clip], jnp.inf)
        send_seg = jnp.where(in_bucket, sorted_seg[src_clip], -1)
        send_rows = jnp.where(in_bucket[..., None], payload[local_order[src_clip]], 0)
        recv_keys = lax.all_to_all(send_keys, 'group', 0, 0, tiled=True)
        recv_seg = lax.all_to_all(send_seg, 'group', 0, 0, tiled=True)
        recv_rows = lax.all_to_all(send_rows, 'group', 0, 0, tiled=True)
        flat_count = group_size * capacity
        flat_pos = jnp.arange(flat_count, dtype=jnp.int32)
        merged_keys, merged_seg, merge_order = lax.sort(
            (recv_keys.reshape(flat_count), recv_seg.reshape(flat_count), flat_pos),
            num_keys=1, is_stable=True)
        merged_rows = recv_rows.reshape(flat_count, width)[merge_order].astype(jnp.float32)
        seg_change = merged_seg[1:] != merged_seg[:-1]
        run_start = jnp.concatenate([jnp.ones((1,), dtype=jnp.bool_), seg_change])
        _, local_scan = lax.associative_scan(combine_runs, (run_start, merged_rows))
        valid_count = jnp.sum(merged_keys < jnp.inf).astype(jnp.int32)
        break_pos = jnp.min(jnp.where(seg_change, flat_pos[1:], flat_count))
        inner_break = (break_pos < valid_count).astype(jnp.int32)
        last_slot = valid_count - 1
        summary_ids = jnp.stack([merged_seg[0], merged_seg[last_slot], inner_break])
        tail_sum = local_scan[last_slot]
        all_ids = lax.all_gather(summary_ids, 'group')
        all_tails = lax.all_gather(tail_sum, 'group')
        first_all = all_ids[:, 0]
        last_all = all_ids[:, 1]
        break_all = all_ids[:, 2]
        dev_ids = jnp.arange(group_size, dtype=jnp.int32)
        link_bad = jnp.concatenate(
            [jnp.ones((1,), jnp.int32), (last_all[:-1] != first_all[1:]).astype(jnp.int32)])
        bad_links = jnp.cumsum(link_bad)
        bad_inner = jnp.cumsum(break_all)
        prev_index = jnp.maximum(my_index - 1, 0)
        carry_mask = (dev_ids < my_index) & (bad_links[my_index] == bad_links) & (bad_inner[prev_index] == bad_inner)
        carry_in = jnp.dot(carry_mask.astype(jnp.float32), all_tails, preferred_element_type=jnp.float32)
        head_run = flat_pos < break_pos
        final_rows = (local_scan + jnp.where(head_run[:, None], carry_in[None, :], 0.0)).astype(jnp.bfloat16)
        _, undo_merge = lax.sort((merge_order, flat_pos), num_keys=1)
        reply = final_rows[undo_merge].reshape(group_size, capacity, width)
        returned = lax.all_to_all(reply, 'group', 0, 0, tiled=True)
        _, sorted_rank = lax.sort((local_order, local_pos), num_keys=1)
        bucket_of = jnp.searchsorted(inner_starts, sorted_rank, side='right').astype(jnp.int32)
        slot_of = bucket_of * capacity + sorted_rank - bucket_start[bucket_of]
        return returned.reshape(flat_count, width)[slot_of]

    row_spec = P(('batch', 'group'))
    mat_spec = P(('batch', 'group'), None)
    return jax.shard_map(per_device, mesh=mesh, in_specs=(row_spec, row_spec, mat_spec),
                         out_specs=mat_spec, check_vma=False)
```

profile of v0, /device:TPU:1, one launch (start us, length us, event | category | flops | bytes accessed | tf_op | source)
XLA Modules:
  0.0 636.0 jit_solution(1080121042130355899)
XLA Ops:
  4.4 45.6 %all-gather = f32[16384,1]{1,0:T(8,128)} all-gather(f32[128,1]{1,0:T(8,128)S(1)} %bitcast.30), channel_id=2, replica_groups=mesh['batch'=1,'group'=128] {'group'}, dimensions={0}, use_global_device_ids=true | all-gather | bytes 66048 | tf_op jit(solution)/shard_map/all_gather | solution.py:26
  54.8 8.7 %sort.88 = (f32[16384]{0:T(1024)S(1)}, s32[16384]{0:T(1024)}) sort(f32[16384]{0:T(1024)S(1)} %reduce, s32[16384]{0:T(1024)S(1)} %iota.39), dimensions={0}, to_apply=%region_1.0 | sort | flops 229376 | bytes 262144 | tf_op jit(solution)/shard_map/jit(sort)/sort | solution.py:27
  63.8 13.7 %while.48 = (s32[]{:T(128)}, u32[127]{0:T(128)S(1)}, u32[127]{0:T(128)S(1)}, f32[127]{0:T(128)S(1)}, pred[127]{0:T(512)(128)(4,1)S(1)}, /*index=5*/f32[512]{0:T(512)S(1)}, s32[]{:T(128)}, s32[]{:T(128)}, s32[]{}) while((s32[]{:T(128)}, u32[127]{0:T(128)S(1)}, u32[127]{0:T(128)S(1)}, f32[127]{0:T(128)S(1)}, ...), condition=%wide.region_3.4_spmd.clone, body=%wide.region_2.3_spmd.clone.sunk | while | flops 5219 | bytes 13230 | solution.py:29
  78.3 6.9 %gather_fusion.4 = f32[1024]{0:T(1024)S(1)} fusion(f32[512]{0:T(512)S(1)} %get-tuple-element.366, s32[1024]{0:T(1024)S(1)} %broadcast_clamp_fusion), kind=kCustom, calls=%fused_computation.4 | custom fusion | bytes 12288 | tf_op jit(solution)/shard_map/gather | solution.py:36
  85.9 5.7 all-to-all-start.1
  91.7 6.9 %gather_fusion.5 = s32[1024]{0:T(1024)S(1)} fusion(s32[512]{0:T(512)S(1)} %get-tuple-element.155, s32[1024]{0:T(1024)S(1)} %broadcast_clamp_fusion), kind=kCustom, calls=%fused_computation.5 | custom fusion | bytes 12288 | tf_op jit(solution)/shard_map/gather | solution.py:37
  98.6 6.9 %gather_fusion.2 = s32[1024]{0:T(1024)S(1)} fusion(s32[512]{0:T(512)S(1)} %get-tuple-element.154, s32[1024]{0:T(1024)S(1)} %broadcast_clamp_fusion), kind=kCustom, calls=%fused_computation.2 | custom fusion | bytes 12288 | tf_op jit(solution)/shard_map/gather | solution.py:38
  106.5 6.0 gather_fusion.3
  112.5 9.8 %all-to-all-start.2 = ((s32[128,1,8]{2,1,0:T(1,128)}), s32[128,1,8]{2,1,0:T(1,128)S(1)}, u32[]{:S(2)}, u32[]{:S(2)}) async-start(s32[128,1,8]{2,1,0:T(1,128)} %bitcast.4), calls=%async_computation.2 | async-start | bytes 131072 | tf_op jit(solution)/shard_map/all_to_all | solution.py:40
  126.8 5.4 all-to-all-done.2
  132.1 5.3 all-to-all-start
  159.6 90.0 %all-reduce.20 = s32[384]{0:T(512)S(1)} all-reduce(s32[384]{0:T(512)S(1)} %add_dynamic-update-slice_fusion), channel_id=3, replica_groups=mesh['batch'=1,'group'=128] {'group'}, use_global_device_ids=true, to_apply=%add.20 | all-reduce | flops 384 | bytes 3072
  258.1 11.6 %gather_fusion.6 = bf16[1024,2048]{1,0:T(8,128)(2,1)} fusion(bf16[1024,2048]{1,0:T(8,128)(2,1)} %bitcast.2, s32[1024]{0:T(1024)S(1)} %fusion.12), kind=kCustom, calls=%fused_computation.6 | custom fusion | bytes 8392704 | tf_op jit(solution)/shard_map/gather | solution.py:47
  270.4 18.2 %slice.273 = f32[512,2048]{1,0:T(8,128)} slice(bf16[1024,2048]{1,0:T(8,128)(2,1)} %gather_fusion.6), slice={[0:1023:2], [0:2048:1]} | slice | bytes 8388608 | tf_op jit(solution)/shard_map/slice | solution.py:50
  288.6 18.2 %slice.272 = f32[512,2048]{1,0:T(8,128)} slice(bf16[1024,2048]{1,0:T(8,128)(2,1)} %gather_fusion.6), slice={[1:1024:2], [0:2048:1]} | slice | bytes 8388608 | tf_op jit(solution)/shard_map/slice | solution.py:50
  306.8 18.5 %slice.270 = f32[511,2048]{1,0:T(8,128)} slice(bf16[1024,2048]{1,0:T(8,128)(2,1)} %gather_fusion.6), slice={[2:1024:2], [0:2048:1]} | slice | bytes 8372224 | tf_op jit(solution)/shard_map/slice | solution.py:50
  331.2 9.8 %slice.280 = f32[256,2048]{1,0:T(8,128)} slice(f32[512,2048]{1,0:T(8,128)} %copy-done.6), slice={[0:511:2], [0:2048:1]} | slice | bytes 4194304 | tf_op jit(solution)/shard_map/slice | solution.py:50
  341.0 9.8 %slice.279 = f32[256,2048]{1,0:T(8,128)} slice(f32[512,2048]{1,0:T(8,128)} %copy-done.6), slice={[1:512:2], [0:2048:1]} | slice | bytes 4194304 | tf_op jit(solution)/shard_map/slice | solution.py:50
  350.8 10.0 %slice.277 = f32[255,2048]{1,0:T(8,128)} slice(f32[512,2048]{1,0:T(8,128)} %copy-done.6), slice={[2:512:2], [0:2048:1]} | slice | bytes 4177920 | tf_op jit(solution)/shard_map/slice | solution.py:50
  392.1 4.8 pad.76
  403.9 16.7 %pad.77 = f32[512,2048]{1,0:T(8,128)} pad(f32[256,2048]{1,0:T(8,128)} %pad_maximum_fusion.1, f32[]{:T(128)} %constant.158.clone.1), padding=0_1_1x0_0_0 | pad | bytes 6291460 | tf_op jit(solution)/shard_map/pad | solution.py:50
  420.7 9.1 %pad.78 = f32[512,2048]{1,0:T(8,128)} pad(f32[256,2048]{1,0:T(8,128)S(1)} %copy-done.11, f32[]{:T(128)} %constant.158.clone.1), padding=1_0_1x0_0_0 | pad | bytes 6291460 | tf_op jit(solution)/shard_map/pad | solution.py:50
  429.7 6.8 %add.293 = f32[512,2048]{1,0:T(8,128)} add(f32[512,2048]{1,0:T(8,128)} %pad.77, f32[512,2048]{1,0:T(8,128)} %pad.78) | non-fusion elementwise | flops 1048576 | bytes 12582912 | tf_op jit(solution)/shard_map/add | solution.py:50
  441.4 32.4 %pad.79 = f32[1024,2048]{1,0:T(8,128)} pad(f32[512,2048]{1,0:T(8,128)} %pad_maximum_fusion, f32[]{:T(128)} %constant.158.clone.1), padding=0_1_1x0_0_0 | pad | bytes 12582916 | tf_op jit(solution)/shard_map/pad | solution.py:50
  473.8 32.5 %pad.80 = f32[1024,2048]{1,0:T(8,128)} pad(f32[512,2048]{1,0:T(8,128)} %add.293, f32[]{:T(128)} %constant.158.clone.1), padding=1_0_1x0_0_0 | pad | bytes 12582916 | tf_op jit(solution)/shard_map/pad | solution.py:50
  507.1 34.4 %all-gather.2 = bf16[128,1,2048]{2,1,0:T(2,128)(2,1)S(1)} all-gather(bf16[1,1,2048]{2,1,0:T(2,128)(2,1)S(1)} %add_bitcast_fusion), channel_id=1, replica_groups=mesh['batch'=1,'group'=128] {'group'}, dimensions={0}, use_global_device_ids=true | all-gather | bytes 528384 | tf_op jit(solution)/shard_map/all_gather | solution.py:58
  542.0 8.6 %add_convert_fusion = bf16[1024,2048]{1,0:T(8,128)(2,1)} fusion(f32[1024,2048]{1,0:T(8,128)} %pad.79, f32[1024,2048]{1,0:T(8,128)} %pad.80, f32[2048]{0:T(1024)S(1)} %bitcast.32, pred[1024]{0:T(1024)(128)(4,1)S(1)} %iota_compare_fusion), kind=kLoop, calls=%fused_computation.28 | loop fusion | flops 8388608 | bytes 20980736 | tf_op jit(solution)/shard_map/convert_element_type | solution.py:71
  550.6 11.6 %gather_fusion.7 = bf16[1024,2048]{1,0:T(8,128)(2,1)} fusion(bf16[1024,2048]{1,0:T(8,128)(2,1)} %add_convert_fusion, s32[1024]{0:T(1024)S(1)} %fusion.13), kind=kCustom, calls=%fused_computation.7 | custom fusion | bytes 8392704 | tf_op jit(solution)/shard_map/gather | solution.py:73
  562.1 7.0 %all-to-all-start.3 = ((bf16[128,8,2048]{2,1,0:T(8,128)(2,1)}), bf16[128,8,2048]{2,1,0:T(8,128)(2,1)}, u32[]{:S(2)}, u32[]{:S(2)}) async-start(bf16[128,8,2048]{2,1,0:T(8,128)(2,1)} %bitcast.29), calls=%async_computation.3 | async-start | bytes 8388608 | tf_op jit(solution)/shard_map/all_to_all | solution.py:74
  569.2 24.1 %while.49 = (s32[]{:T(128)}, u32[512]{0:T(512)S(1)}, u32[512]{0:T(512)S(1)}, s32[127]{0:T(128)S(1)}, s32[512]{0:T(512)S(1)}, /*index=5*/s32[]{:T(128)}, s32[]{:T(128)}, s32[]{}) while((s32[]{:T(128)}, u32[512]{0:T(512)S(1)}, u32[512]{0:T(512)S(1)}, s32[127]{0:T(128)S(1)}, s32[512]{0:T(512)S(1)}, /*index=5*/s32[]{:T(128)}, ...), condition=%wide.region_12.13_spmd.clone, body=%wide.region_11.12_spmd.clone.sunk | while | flops 10244 | bytes 40045 | solution.py:76
  596.7 31.0 %all-to-all-done.3 = bf16[128,8,2048]{2,1,0:T(8,128)(2,1)} async-done(((bf16[128,8,2048]{2,1,0:T(8,128)(2,1)}), bf16[128,8,2048]{2,1,0:T(8,128)(2,1)}, u32[]{:S(2)}, u32[]{:S(2)}) %all-to-all-start.3) | async-done | bytes 4194336 | tf_op jit(solution)/shard_map/all_to_all | solution.py:74
  627.7 8.1 %gather_fusion.9 = bf16[512,2048]{1,0:T(8,128)(2,1)} fusion(bf16[1024,2048]{1,0:T(8,128)(2,1)} %bitcast.15, s32[1024]{0:T(1024)S(1)} %pad_clamp_fusion.2), kind=kCustom, calls=%fused_computation.9 | custom fusion | bytes 4196352 | tf_op jit(solution)/shard_map/gather | solution.py:78
  (316 shorter events, 135.4 us)
Async XLA Ops:
  0.0 106.5 %copy-start = (bf16[512,2048]{1,0:T(8,128)(2,1)S(1)}, bf16[512,2048]{1,0:T(8,128)(2,1)}, u32[]{:S(2)}) copy-start(bf16[512,2048]{1,0:T(8,128)(2,1)} %param.9) | copy-start | bytes 6291460
  77.4 0.5 copy-start.2
  85.9 26.6 %all-to-all-start.1 = ((f32[128,1,8]{2,1,0:T(1,128)}), f32[128,1,8]{2,1,0:T(1,128)S(1)}, u32[]{:S(2)}, u32[]{:S(2)}) async-start(f32[128,1,8]{2,1,0:T(1,128)} %bitcast.3), calls=%async_computation.1 | async-start | bytes 131072 | tf_op jit(solution)/shard_map/all_to_all | solution.py:39
  112.5 19.6 %all-to-all-start.2 = ((s32[128,1,8]{2,1,0:T(1,128)}), s32[128,1,8]{2,1,0:T(1,128)S(1)}, u32[]{:S(2)}, u32[]{:S(2)}) async-start(s32[128,1,8]{2,1,0:T(1,128)} %bitcast.4), calls=%async_computation.2 | async-start | bytes 131072 | tf_op jit(solution)/shard_map/all_to_all | solution.py:40
  132.1 125.9 %all-to-all-start = ((bf16[128,8,2048]{2,1,0:T(8,128)(2,1)}), bf16[128,8,2048]{2,1,0:T(8,128)(2,1)}, u32[]{:S(2)}, u32[]{:S(2)}) async-start(bf16[128,8,2048]{2,1,0:T(8,128)(2,1)} %bitcast_select_fusion), calls=%async_computation | async-start | bytes 8388608 | tf_op jit(solution)/shard_map/all_to_all | solution.py:41
  329.2 2.0 copy-start.6
  363.3 10.4 %copy-start.10 = (f32[256,2048]{1,0:T(8,128)}, f32[256,2048]{1,0:T(8,128)S(1)}, u32[]{:S(2)}) copy-start(f32[256,2048]{1,0:T(8,128)S(1)} %add_select_fusion.3) | copy-start | bytes 6291460
  373.8 4.3 copy-start.13
  380.4 1.5 slice-start.2
  382.1 4.7 slice-start.1
  386.8 5.3 copy-start.14
  392.1 4.9 copy-start.7
  396.9 3.4 copy-start.8
  396.9 3.4 copy-start.12
  400.4 2.0 slice-start
  403.9 16.7 %copy-start.11 = (f32[256,2048]{1,0:T(8,128)S(1)}, f32[256,2048]{1,0:T(8,128)}, u32[]{:S(2)}) copy-start(f32[256,2048]{1,0:T(8,128)} %add.291) | copy-start | bytes 6291460
  429.7 6.8 %copy-start.4 = (f32[512,2048]{1,0:T(8,128)S(1)}, f32[512,2048]{1,0:T(8,128)}, u32[]{:S(2)}) copy-start(f32[512,2048]{1,0:T(8,128)} %pad.77) | copy-start | bytes 12582916
  429.7 6.8 %copy-start.5 = (f32[512,2048]{1,0:T(8,128)S(1)}, f32[512,2048]{1,0:T(8,128)}, u32[]{:S(2)}) copy-start(f32[512,2048]{1,0:T(8,128)} %pad.78) | copy-start | bytes 12582916
  429.7 8.6 %copy-start.9 = (f32[511,2048]{1,0:T(8,128)S(1)}, f32[511,2048]{1,0:T(8,128)}, u32[]{:S(2)}) copy-start(f32[511,2048]{1,0:T(8,128)} %slice.270) | copy-start | bytes 12558340
  562.1 7.0 %copy-start.3 = (s32[127]{0:T(128)S(1)}, s32[127]{0:T(128)}, u32[]{:S(2)}) copy-start(s32[127]{0:T(128)} %copy-done.2) | copy-start | bytes 1528
  562.1 65.6 %all-to-all-start.3 = ((bf16[128,8,2048]{2,1,0:T(8,128)(2,1)}), bf16[128,8,2048]{2,1,0:T(8,128)(2,1)}, u32[]{:S(2)}, u32[]{:S(2)}) async-start(bf16[128,8,2048]{2,1,0:T(8,128)(2,1)} %bitcast.29), calls=%async_computation.3 | async-start | bytes 8388608 | tf_op jit(solution)/shard_map/all_to_all | solution.py:74
  627.7 8.1 %copy-start.1 = (bf16[512,2048]{1,0:T(8,128)(2,1)S(1)}, bf16[512,2048]{1,0:T(8,128)(2,1)}, u32[]{:S(2)}) copy-start(bf16[512,2048]{1,0:T(8,128)(2,1)} %param.9) | copy-start | bytes 6291460
where the time goes:
time: 646 us; the launch traced here: 636 us
  local copies, waits for them, and re-layouts  310 us (48%)
  blocking collectives  170 us (26%)
  other arithmetic  86.7 us (13%)
  waiting for transfers between devices  36.4 us (6%)
  starting transfers between devices  27.7 us (4%)
    slice x65, local copies, waits for them, and re-layouts, per_device(): _, local_scan = lax.associative_scan(combine_runs, (run_start, merged_rows))  102 us
    pad x18, local copies, waits for them, and re-layouts, per_device(): _, local_scan = lax.associative_scan(combine_runs, (run_start, merged_rows))  102 us
    unnamed x1, blocking collectives  90 us
    all_gather x1, blocking collectives, per_device(): all_samples = lax.all_gather(samples, 'group', tiled=True)  45.6 us
    all_gather x1, blocking collectives, per_device(): all_tails = lax.all_gather(tail_sum, 'group')  34.4 us
    all_to_all x1, waiting for transfers between devices, per_device(): returned = lax.all_to_all(reply, 'group', 0, 0, tiled=True)  31 us
    gather x7, local copies, waits for them, and re-layouts, per_device(): jnp.searchsorted(inner_starts, sorted_rank, side='right').astype(jnp.int32)  23.4 us
    select_n x17, other arithmetic, combine_runs(): jnp.where(right_flag[..., None], right_rows, left_rows + right_rows)  14.3 us
  transfers between devices with their start and end apart: 4, of which 2 were waited for; matrix products, arithmetic and copies ran while one was open for 13% of the time, Pallas kernels for 0%

commit v1 on v0

v1 whole, which is shorter than its diff:
```python
import functools

import jax
import jax.numpy as jnp
from jax import lax
from jax.experimental import pallas as pl
from jax.experimental.pallas import tpu as pltpu
from jax.sharding import PartitionSpec as P

F32 = jnp.float32
BF16 = jnp.bfloat16
I32 = jnp.int32
NEG = float('-inf')
POS = float('inf')

DEVS = 128
ROWS = 512
WIDTH = 2048
SPLIT = 2
CAP = 8 * SPLIT
GROUPS = DEVS // SPLIT
COLS = WIDTH // SPLIT
PACK = GROUPS * CAP
SLOTS = DEVS * CAP
TAILW = COLS + 128


def iota(shape, dim):
    return lax.broadcasted_iota(I32, shape, dim)


def peer(me, idx):
    core, x, y, z = me % 2, (me // 2) % 4, (me // 8) % 4, me // 32
    blk, turn, flip = idx // 8, (idx // 2) % 4, idx % 2
    dst_x = (x + turn) % 4
    dst_y = (y + turn + blk % 4) % 4
    dst_z = (z + turn + blk // 4) % 4
    return ((dst_z * 4 + dst_y) * 4 + dst_x) * 2 + (core + flip) % 2


def kernel(keys_ref, segs_ref, pay_ref, out_ref, samp_msg, samp_all, packed, recv, meta_msg, meta_all, mask_ref,
           kcol_ref, scol_ref, bcol_ref, krow_ref, srow_ref, tail_msg, tail_all, sums_ref, ret, send_sem, samp_sem,
           meta_sem, row_sem, tail_sem, ret_sem):
    me = lax.axis_index('group')
    my_group = me // SPLIT
    my_part = me % SPLIT
    barrier = pltpu.get_barrier_semaphore()

    def remote(src, dst, recv_sem, dev):
        return pltpu.make_async_remote_copy(src_ref=src, dst_ref=dst, send_sem=send_sem, recv_sem=recv_sem,
                                            device_id={'group': dev}, device_id_type=pl.DeviceIdType.MESH)

    def each_peer(fn):
        def step(idx, carry):
            fn(peer(me, idx))
            return carry
        lax.fori_loop(1, DEVS, step, 0)

    each_peer(lambda dev: pl.semaphore_signal(barrier, inc=1, device_id={'group': dev},
                                              device_id_type=pl.DeviceIdType.MESH))

    key_row = keys_ref[...]
    seg_row = segs_ref[...]
    eye = iota((ROWS, ROWS), 0) == iota((ROWS, ROWS), 1)

    def to_col(row):
        return jnp.sum(jnp.where(eye, jnp.broadcast_to(row, (ROWS, ROWS)), 0), axis=1, keepdims=True)

    def to_row(col):
        return jnp.sum(jnp.where(eye, jnp.broadcast_to(col, (ROWS, ROWS)), 0), axis=0, keepdims=True)

    key_col = to_col(key_row)
    rank_col = jnp.sum(jnp.where(key_row < key_col, 1.0, 0.0), axis=1, keepdims=True)
    quad = iota((ROWS, DEVS), 1).astype(F32) * 4.0
    samp_msg[...] = jnp.sum(jnp.where(rank_col == quad, jnp.broadcast_to(key_col, (ROWS, DEVS)), 0.0), axis=0,
                            keepdims=True)
    pl.semaphore_wait(barrier, DEVS - 1)

    each_peer(lambda dev: remote(samp_msg, samp_all.at[me], samp_sem, dev).start())
    samp_all[me] = samp_msg[...]
    remote(samp_all.at[pl.ds(0, DEVS - 1)], samp_all.at[pl.ds(0, DEVS - 1)], samp_sem, me).wait_recv()

    counts = []
    for part in range(ROWS // 128):
        kblk = jnp.broadcast_to(key_col[part * 128:(part + 1) * 128], (128, 128))

        def count(step, acc, kblk=kblk):
            for sub in range(8):
                acc = acc + jnp.where(samp_all[step * 8 + sub] <= kblk, 1.0, 0.0)
            return acc

        acc = lax.fori_loop(0, DEVS // 8, count, jnp.zeros((128, 128), F32))
        counts.append(jnp.sum(acc, axis=1, keepdims=True))
    seen_col = jnp.concatenate(counts, axis=0)
    group_col = jnp.maximum(jnp.floor((seen_col - (DEVS // 2 + 1)) * (1.0 / (DEVS * SPLIT))), 0.0)
    group_row = to_row(group_col)
    slot_col = rank_col - jnp.sum(jnp.where(group_row < group_col, 1.0, 0.0), axis=1, keepdims=True)
    place_col = group_col * CAP + slot_col
    place_row = to_row(place_col)

    hi_row = (seg_row // 65536).astype(F32)
    lo_row = (seg_row % 65536).astype(F32)
    pack_blk = 256

    def pack(step, carry):
        base = step * pack_blk
        hit = place_row == (iota((pack_blk, ROWS), 0) + base).astype(F32)
        slot = iota((pack_blk, 128), 0) % CAP
        lane = iota((pack_blk, 128), 1)
        spread = jnp.zeros((pack_blk, 128), F32)
        for no, val in enumerate((key_row, hi_row, lo_row, jnp.ones((1, ROWS), F32))):
            got = jnp.sum(jnp.where(hit, jnp.broadcast_to(val, (pack_blk, ROWS)), 0.0), axis=1, keepdims=True)
            spread = spread + jnp.where(lane == slot + no * CAP, got, 0.0)
        meta = jnp.sum(spread.reshape(pack_blk // CAP, CAP, 128), axis=1, keepdims=True)
        meta_msg[pl.ds(step * (pack_blk // CAP), pack_blk // CAP)] = meta
        hot = jnp.where(hit, 1.0, 0.0).astype(BF16)
        for part in range(SPLIT):
            rows = jnp.dot(hot, pay_ref[:, part * COLS:(part + 1) * COLS], preferred_element_type=F32)
            packed[part, pl.ds(pl.multiple_of(base, pack_blk), pack_blk)] = rows.astype(BF16)
        return carry

    lax.fori_loop(0, PACK // pack_blk, pack, 0)

    def my_rows(dev):
        return pl.ds(pl.multiple_of(dev * CAP, CAP), CAP)

    each_peer(lambda dev: remote(meta_msg.at[dev // SPLIT], meta_all.at[me], meta_sem, dev).start())
    each_peer(lambda dev: remote(packed.at[dev % SPLIT, my_rows(dev // SPLIT)], recv.at[my_rows(me)], row_sem, dev).start())
    meta_all[me] = meta_msg[my_group]
    recv[my_rows(me)] = packed[my_part, my_rows(my_group)]
    remote(meta_all.at[pl.ds(0, DEVS - 1)], meta_all.at[pl.ds(0, DEVS - 1)], meta_sem, me).wait_recv()

    col_blk = 128

    def columns(step, carry):
        got = meta_all[pl.ds(step * (col_blk // CAP), col_blk // CAP)]
        got = jnp.broadcast_to(got, (col_blk // CAP, CAP, 128)).reshape(col_blk, 128)
        slot = iota((col_blk, 128), 0) % CAP
        lane = iota((col_blk, 128), 1)
        vals = [jnp.sum(jnp.where(lane == slot + no * CAP, got, 0.0), axis=1, keepdims=True) for no in range(4)]
        live = vals[3] > 0.0
        seg = vals[1].astype(I32) * 65536 + vals[2].astype(I32)
        rows = pl.ds(pl.multiple_of(step * col_blk, col_blk), col_blk)
        kcol_ref[rows] = jnp.broadcast_to(jnp.where(live, vals[0], NEG), (col_blk, 128))
        scol_ref[rows] = jnp.broadcast_to(seg, (col_blk, 128))
        diag = iota((col_blk, 128), 0) == lane
        krow_ref[step] = jnp.sum(jnp.where(diag, jnp.where(live, vals[0], POS), 0.0), axis=0, keepdims=True)
        srow_ref[step] = jnp.sum(jnp.where(diag, seg, 0), axis=0, keepdims=True)
        return carry

    lax.fori_loop(0, SLOTS // col_blk, columns, 0)
    tiles = SLOTS // 128
    krow = [krow_ref[t] for t in range(tiles)]
    srow = [srow_ref[t] for t in range(tiles)]

    def masks(step, carry):
        rows = my_rows(step)
        kcol = kcol_ref[rows]
        scol = scol_ref[rows]
        best = jnp.full((CAP, 128), NEG, F32)
        for t in range(tiles):
            best = jnp.maximum(best, jnp.where((krow[t] < kcol) & (srow[t] != scol), krow[t], NEG))
        bound = jnp.broadcast_to(jnp.max(best, axis=1, keepdims=True), (CAP, 128))
        bcol_ref[rows] = bound
        for t in range(tiles):
            take = (krow[t] > bound) & (krow[t] <= kcol)
            mask_ref[rows, t * 128:(t + 1) * 128] = jnp.where(take, 1.0, 0.0).astype(BF16)
        return carry

    lax.fori_loop(0, DEVS, masks, 0)

    def over(vals, fold, red):
        acc = vals[0]
        for val in vals[1:]:
            acc = fold(acc, val)
        return red(acc, axis=1, keepdims=True)

    live_max = [jnp.where(k < POS, k, NEG) for k in krow]
    key_last = over(live_max, jnp.maximum, jnp.max)
    key_first = over(krow, jnp.minimum, jnp.min)
    hi_of = [(s // 65536).astype(F32) for s in srow]
    lo_of = [(s % 65536).astype(F32) for s in srow]

    def pick(key, vals):
        return over([jnp.where(k == key, v, 0.0) for k, v in zip(krow, vals)], jnp.add, jnp.sum)

    last_hi, last_lo = pick(key_last, hi_of), pick(key_last, lo_of)
    first_hi, first_lo = pick(key_first, hi_of), pick(key_first, lo_of)
    cut = over([jnp.where((k < POS) & ((h != last_hi) | (l != last_lo)), k, NEG)
                for k, h, l in zip(krow, hi_of, lo_of)], jnp.maximum, jnp.max)
    tail_hot = jnp.concatenate([jnp.where((k > cut) & (k < POS), 1.0, 0.0) for k in krow], axis=1)
    tail_hot = jnp.broadcast_to(tail_hot, (16, SLOTS)).astype(BF16)
    lane = iota((1, 128), 1)
    facts = jnp.zeros((1, 128), F32)
    for no, val in enumerate((first_hi, first_lo, last_hi, last_lo, jnp.where(cut > NEG, 1.0, 0.0))):
        facts = jnp.where(lane == no, val, facts)

    remote(recv.at[pl.ds(0, SLOTS - CAP)], recv.at[pl.ds(0, SLOTS - CAP)], row_sem, me).wait_recv()
    tail = jnp.dot(tail_hot, recv[...], preferred_element_type=F32)[0:1]
    tail_msg[:, :COLS] = tail
    tail_msg[:, COLS:] = facts

    def send_tail(step, carry):
        dst_group = (my_group + step) % GROUPS
        remote(tail_msg, tail_all.at[my_group], tail_sem, dst_group * SPLIT + my_part).start()
        return carry

    lax.fori_loop(1, GROUPS, send_tail, 0)
    tail_all[my_group] = tail_msg[...]
    remote(tail_all.at[pl.ds(0, GROUPS - 1)], tail_all.at[pl.ds(0, GROUPS - 1)], tail_sem, me).wait_recv()

    all_facts = tail_all[:, 0, COLS:]
    lanes = iota((GROUPS, 128), 1)

    def fact(no):
        return jnp.sum(jnp.where(lanes == no, all_facts, 0.0), axis=1, keepdims=True)

    group_no = iota((GROUPS, 1), 0)
    before = group_no < my_group
    same_first = (fact(0) == first_hi) & (fact(1) == first_lo)
    same_last = (fact(2) == first_hi) & (fact(3) == first_lo)
    stop = before & ((fact(4) > 0.0) | jnp.logical_not(same_first))
    last_stop = jnp.max(jnp.where(stop, group_no, -1), axis=0, keepdims=True)
    linked = before & ((group_no > last_stop) | ((group_no == last_stop) & same_last))
    carry_in = jnp.sum(jnp.where(linked, tail_all[:, 0, :COLS], 0.0), axis=0, keepdims=True)

    def sums(blk, carry):
        devs = [peer(me, blk * 8 + sub) for sub in range(8)]
        hot = jnp.concatenate([mask_ref[my_rows(dev)] for dev in devs], axis=0)
        bound = jnp.concatenate([bcol_ref[my_rows(dev)] for dev in devs], axis=0)
        open_run = bound[:, :1] == NEG
        total = jnp.dot(hot, recv[...], preferred_element_type=F32)
        total = (total + jnp.where(open_run, carry_in, 0.0)).astype(BF16)
        for sub, dev in enumerate(devs):
            sums_ref[my_rows(dev)] = total[sub * CAP:(sub + 1) * CAP]
            send = remote(sums_ref.at[my_rows(dev)], ret.at[my_part, my_rows(my_group)], ret_sem, dev)
            if sub == 0:
                @pl.when(blk > 0)
                def _(send=send):
                    send.start()
            else:
                send.start()
        return carry

    lax.fori_loop(0, DEVS // 8, sums, 0)
    ret[my_part, my_rows(my_group)] = sums_ref[my_rows(me)]
    remote(recv.at[pl.ds(0, SLOTS - CAP)], recv.at[pl.ds(0, SLOTS - CAP)], ret_sem, me).wait_recv()

    def unpack(step, carry):
        spot = iota((128, PACK), 1).astype(F32)
        for blk in range(ROWS // 128):
            hot = jnp.where(spot == place_col[blk * 128:(blk + 1) * 128], 1.0, 0.0).astype(BF16)
            for part in range(SPLIT):
                rows = jnp.dot(hot, ret[part], preferred_element_type=F32)
                out_ref[blk * 128:(blk + 1) * 128, part * COLS:(part + 1) * COLS] = rows.astype(BF16)
        return carry

    unpack(0, 0)

    def sent(src):
        remote(src, src, ret_sem, me).wait_send()

    sent(samp_all.at[pl.ds(0, DEVS - 1)])
    sent(meta_all.at[pl.ds(0, DEVS - 1)])
    sent(recv.at[pl.ds(0, SLOTS - CAP)])
    sent(tail_all.at[pl.ds(0, GROUPS - 1)])
    sent(recv.at[pl.ds(0, SLOTS - CAP)])


def solution(mesh):
    def per_device(sort_keys, seg_ids, payload):
        vmem = pl.BlockSpec(memory_space=pltpu.VMEM)
        dma = pltpu.SemaphoreType.DMA
        call = pl.pallas_call(
            kernel,
            out_shape=jax.ShapeDtypeStruct((ROWS, WIDTH), BF16),
            in_specs=[vmem] * 3,
            out_specs=vmem,
            scratch_shapes=[
                pltpu.VMEM((1, DEVS), F32),
                pltpu.VMEM((DEVS, 1, DEVS), F32),
                pltpu.VMEM((SPLIT, PACK, COLS), BF16),
                pltpu.VMEM((SLOTS, COLS), BF16),
                pltpu.VMEM((GROUPS, 1, 128), F32),
                pltpu.VMEM((DEVS, 1, 128), F32),
                pltpu.VMEM((SLOTS, SLOTS), BF16),
                pltpu.VMEM((SLOTS, 128), F32),
                pltpu.VMEM((SLOTS, 128), I32),
                pltpu.VMEM((SLOTS, 128), F32),
                pltpu.VMEM((SLOTS // 128, 1, 128), F32),
                pltpu.VMEM((SLOTS // 128, 1, 128), I32),
                pltpu.VMEM((1, TAILW), F32),
                pltpu.VMEM((GROUPS, 1, TAILW), F32),
                pltpu.VMEM((SLOTS, COLS), BF16),
                pltpu.VMEM((SPLIT, PACK, COLS), BF16),
                dma, dma, dma, dma, dma, dma,
            ],
            compiler_params=pltpu.CompilerParams(collective_id=0, has_side_effects=True, vmem_limit_bytes=62 << 20),
        )
        return call(sort_keys.reshape(1, ROWS), seg_ids.reshape(1, ROWS), payload)

    row_spec = P(('batch', 'group'))
    mat_spec = P(('batch', 'group'), None)
    return jax.shard_map(per_device, mesh=mesh, in_specs=(row_spec, row_spec, mat_spec),
                         out_specs=mat_spec, check_vma=False)
```

time: 646 us -> 179 us (0.28); the launches traced: 636 us -> 177 us
  local copies, waits for them, and re-layouts: 310 us -> 3.16 us
  Pallas kernels: 0 us -> 173 us
  blocking collectives: 170 us -> 0 us
  other arithmetic: 86.7 us -> 0 us
  waiting for transfers between devices: 36.4 us -> 0 us
  starting transfers between devices: 27.7 us -> 0 us
    pallas_call x0 -> x1, Pallas kernels: none -> 173 us  [per_device(): return call(sort_keys.reshape(1, ROWS), seg_ids.reshape(1, ROWS), payload)]
    slice x68 -> x0, local copies, waits for them, and re-layouts: 103 us -> none  [the longest x65 102 us: per_device(): _, local_scan = lax.associative_scan(combine_runs, (run_start, merged_rows))]
    pad x18 -> x0, local copies, waits for them, and re-layouts: 102 us -> none  [per_device(): _, local_scan = lax.associative_scan(combine_runs, (run_start, merged_rows))]
    gather x28 -> x0, local copies, waits for them, and re-layouts: 97.5 us -> none  [the longest x7 23.4 us: per_device(): jnp.searchsorted(inner_starts, sorted_rank, side='right').astype(jnp.int32)]
    unnamed x1 -> x0, blocking collectives: 90 us -> none
    all_gather x2 -> x0, blocking collectives: 80.1 us -> none  [the longest x1 45.6 us: per_device(): all_samples = lax.all_gather(samples, 'group', tiled=True)]
    all_to_all x4 -> x0, waiting for transfers between devices: 36.4 us -> none  [the longest x1 31 us: per_device(): returned = lax.all_to_all(reply, 'group', 0, 0, tiled=True)]
    all_to_all x4 -> x0, starting transfers between devices: 27.7 us -> none  [the longest x1 9.76 us: per_device(): recv_seg = lax.all_to_all(send_seg, 'group', 0, 0, tiled=True)]
  transfers between devices with their start and end apart: 4 -> 0, of which waited for: 2 -> 0; matrix products, arithmetic and copies ran while one was open for 13% -> 0% of each run, Pallas kernels for 0% -> 0%
where the time goes in v1:
time: 179 us; the launch traced here: 177 us
  Pallas kernels  173 us (97%)
  local copies, waits for them, and re-layouts  3.16 us (2%)
    pallas_call x1, Pallas kernels, per_device(): return call(sort_keys.reshape(1, ROWS), seg_ids.reshape(1, ROWS), payload)  173 us

profile of v1, /device:TPU:1, one launch (start us, length us, event | category | flops | bytes accessed | tf_op | source)
XLA Modules:
  0.0 176.6 jit_solution(11290056192585214232)
XLA Ops:
  0.0 173.4 %shard_map.37 = bf16[512,2048]{1,0:T(8,128)(2,1)} custom-call(f32[1,512]{1,0:T(1,128)} %bitcast.2, s32[1,512]{1,0:T(1,128)} %bitcast.3, bf16[512,2048]{1,0:T(8,128)(2,1)} %pay_ref.1), custom_call_target="tpu_custom_call" | custom-call | tf_op jit(solution)/shard_map/pallas_call | solution.py:300
  173.4 3.2 %copy.5 = bf16[512,2048]{1,0:T(8,128)(2,1)} copy(bf16[512,2048]{1,0:T(8,128)(2,1)} %shard_map.37) | data formatting | bytes 4194304

commit v2 on v0

v2 whole, which is shorter than its diff:
```python
import functools

import jax
import jax.numpy as jnp
from jax import lax
from jax.experimental import pallas as pl
from jax.experimental.pallas import tpu as pltpu
from jax.sharding import PartitionSpec as P

F32 = jnp.float32
BF16 = jnp.bfloat16
I32 = jnp.int32
NEG = float('-inf')
POS = float('inf')
MESH = pl.DeviceIdType.MESH

DEVS = 128
ROWS = 512
WIDTH = 2048
LANES = 128
BASE = 16
MORE = 4
FLAG = LANES - 1
HALF = 65536
TALL = 32
RING = 4


class Plan:
    def __init__(self, parts, more):
        self.parts, self.more = parts, more
        self.shift = parts.bit_length() - 1
        self.ranges = DEVS // parts
        self.cols = WIDTH // parts
        self.chunks = self.cols // LANES
        self.full = BASE + more
        self.line = self.cols + (LANES if more else 0)
        self.low = DEVS * BASE
        self.top = DEVS * more
        self.need = self.low + self.top
        self.low_out = self.ranges * BASE
        self.top_out = self.ranges * more
        self.tail = self.cols + LANES


NARROW = Plan(4, MORE)
FULL = Plan(2, 0)


def iota(shape, dim):
    return lax.broadcasted_iota(I32, shape, dim)


def ones_where(hit):
    return jnp.where(hit, 1.0, 0.0)


def hot(hit):
    return ones_where(hit).astype(BF16)


def dot(left, right):
    return jnp.dot(left, right, preferred_element_type=F32)


def along_sublanes(vals):
    return jnp.sum(vals, axis=0, keepdims=True)


def along_lanes(vals):
    return jnp.sum(vals, axis=1, keepdims=True)


def place(me, step):
    core, x, y, z = me & 1, (me >> 1) & (RING - 1), (me >> 3) & (RING - 1), me >> 5
    return (core + step) & 1, ((x + step) & (RING - 1)) << 1, ((y + step) & (RING - 1)) << 3, ((z + step) & (RING - 1)) << 5


def block_of_eight(me, blk):
    found = []
    for turn in range(RING):
        side = place(me, turn)[1] + place(me, turn + (blk & (RING - 1)))[2] + place(me, turn + (blk >> 2))[3]
        found += [side + place(me, flip)[0] for flip in range(2)]
    return found


def kernel(plan, keys_ref, segs_ref, pay_ref, out_ref, flag_ref, samp_msg, samp_all, packed, recv, meta_msg, meta_all,
           mask_ref, kcol_ref, scol_ref, bcol_ref, krow_ref, srow_ref, tail_msg, tail_all, top_ref, sums_ref, ret,
           back_ref, send_sem, samp_sem, meta_sem, row_sem, tail_sem, ret_sem):
    parts, more, cols, chunks = plan.parts, plan.more, plan.cols, plan.chunks
    me = lax.axis_index('group')
    my_range = me >> plan.shift
    my_part = me & (parts - 1)
    barrier = pltpu.get_barrier_semaphore()
    others = [dev for blk in range(DEVS // 8) for dev in block_of_eight(me, blk)][1:]
    rest = pl.ds(0, DEVS - 1)
    most = pl.ds(0, plan.low - BASE)

    def remote(src, dst, recv_sem, dev):
        return pltpu.make_async_remote_copy(src_ref=src, dst_ref=dst, send_sem=send_sem, recv_sem=recv_sem,
                                            device_id={'group': dev}, device_id_type=MESH)

    def arrived(like, sem):
        remote(like, like, sem, others[0]).wait_recv()

    def left(like):
        remote(like, like, ret_sem, others[0]).wait_send()

    def at16(no):
        return pl.ds(pl.multiple_of(no * BASE, BASE), BASE)

    for dev in others:
        pl.semaphore_signal(barrier, inc=1, device_id={'group': dev}, device_id_type=MESH)

    key_row = keys_ref[...]
    seg_row = segs_ref[...]
    square = (ROWS, ROWS)
    eye = iota(square, 0) == iota(square, 1)

    def to_col(row):
        return along_lanes(jnp.where(eye, jnp.broadcast_to(row, square), 0))

    def to_row(col):
        return along_sublanes(jnp.where(eye, jnp.broadcast_to(col, square), 0))

    key_col = to_col(key_row)
    seg_col = to_col(seg_row)
    rank_col = along_lanes(ones_where(key_row < key_col))
    wide = (ROWS, LANES)
    fourth = (iota(wide, 1) * (ROWS // DEVS)).astype(F32)
    samp_msg[...] = along_sublanes(jnp.where(rank_col == fourth, jnp.broadcast_to(key_col, wide), 0.0))
    pl.semaphore_wait(barrier, DEVS - 1)

    for dev in others:
        remote(samp_msg, samp_all.at[me], samp_sem, dev).start()
    samp_all[me] = samp_msg[...]
    arrived(samp_all.at[rest], samp_sem)

    tile = (LANES, LANES)
    counts = []
    for part in range(ROWS // LANES):
        kblk = jnp.broadcast_to(key_col[part * LANES:(part + 1) * LANES], tile)

        def count(step, acc, kblk=kblk):
            for sub in range(8):
                acc = acc + ones_where(samp_all[step * 8 + sub] <= kblk)
            return acc

        counts.append(along_lanes(lax.fori_loop(0, DEVS // 8, count, jnp.zeros(tile, F32))))
    seen_col = jnp.concatenate(counts, axis=0)
    range_col = jnp.maximum(jnp.floor((seen_col - (DEVS // 2 + 1)) * (1.0 / (DEVS * parts))), 0.0)
    range_row = to_row(range_col)
    slot_col = rank_col - along_lanes(ones_where(range_row < range_col))
    low_col = jnp.where(slot_col < BASE, range_col * BASE + slot_col, -1.0)
    low_row = to_row(low_col)
    top_col = jnp.where((slot_col >= BASE) & (slot_col < plan.full), range_col * more + (slot_col - BASE), -1.0)
    spill = ones_where(jnp.max(slot_col, axis=0, keepdims=True) >= plan.full)

    lane = iota(wide, 1)
    lane_val = lane // plan.full
    lane_slot = (lane % plan.full).astype(F32)
    vals = jnp.where(lane_val == 0, key_col, 1.0)
    vals = jnp.where(lane_val == 1, (seg_col // HALF).astype(F32), vals)
    vals = jnp.where(lane_val == 2, (seg_col % HALF).astype(F32), vals)
    vals = jnp.where((lane_slot == slot_col) & (lane_val < 4), vals, 0.0)
    range_b = jnp.broadcast_to(range_col, wide)
    lane_one = iota((1, LANES), 1)
    for dst in range(plan.ranges):
        meta = along_sublanes(jnp.where(range_b == float(dst), vals, 0.0))
        meta_msg[dst] = jnp.where(lane_one == FLAG, spill, meta)
    for dev in others:
        remote(meta_msg.at[dev >> plan.shift], meta_all.at[me], meta_sem, dev).start()
    meta_all[me] = meta_msg[my_range]

    def fold(to, groups):
        return ((to % BASE) // MORE) * groups + (to // BASE) * MORE + to % MORE

    lines = (plan.low_out, plan.low_out)
    hot_low = hot(low_row == iota((plan.low_out, ROWS), 0).astype(F32))
    if more:
        hot_top = hot(to_row(top_col) == iota((plan.top_out, ROWS), 0).astype(F32))
    piles = []
    for part in range(parts):
        pay = pay_ref[:, part * cols:(part + 1) * cols]
        packed[part, :, :cols] = dot(hot_low, pay).astype(BF16)
        if more:
            rows = dot(hot_top, pay).astype(BF16)
            piles.append(jnp.concatenate([rows[:, c * LANES:(c + 1) * LANES] for c in range(chunks)], axis=0))
    if more:
        folded = dot(hot(iota(lines, 1) == fold(iota(lines, 0), plan.top_out)), jnp.concatenate(piles, axis=1)).astype(BF16)
        for part in range(parts):
            packed[part, :, cols:] = folded[:, part * LANES:(part + 1) * LANES]
    for dev in others:
        remote(packed.at[dev & (parts - 1), at16(dev >> plan.shift)], recv.at[at16(me)], row_sem, dev).start()
    recv[at16(me)] = packed[my_part, at16(my_range)]
    arrived(meta_all.at[rest], meta_sem)

    low_tiles = plan.low // LANES
    tiles = plan.need // LANES
    each = LANES // BASE
    quarters = BASE // MORE
    sub = iota(tile, 0)
    lanes = iota(tile, 1)
    diag = sub == lanes

    def read_slots(got, slot):
        found = [along_lanes(jnp.where(lanes == slot + no * plan.full, got, 0.0)) for no in range(4)]
        seg = found[1].astype(I32) * HALF + found[2].astype(I32)
        return found[3] > 0.0, found[0], seg

    def keep(step, live, key, seg):
        rows = pl.ds(step * LANES, LANES)
        kcol_ref[rows] = jnp.broadcast_to(jnp.where(live, key, NEG), tile)
        scol_ref[rows] = jnp.broadcast_to(seg, tile)

    def to_lanes(spot, live, key, seg):
        return along_sublanes(jnp.where(spot, jnp.where(live, key, POS), 0.0)), along_sublanes(jnp.where(spot, seg, 0))

    top_keys, top_segs = [], []
    for step in range(low_tiles):
        got = meta_all[step * each:(step + 1) * each]
        got = jnp.broadcast_to(got, (each, BASE, LANES)).reshape(tile)
        slots = read_slots(got, sub % BASE)
        keep(step, *slots)
        krow_ref[step], srow_ref[step] = to_lanes(diag, *slots)
        if more:
            first = (step % quarters) * (LANES // quarters)
            spot = (sub % BASE < MORE) & (lanes == first + (sub // BASE) * MORE + sub % MORE)
            key, seg = to_lanes(spot, *read_slots(got, BASE + sub % MORE))
            top_keys.append(key)
            top_segs.append(seg)
    for no in range(tiles - low_tiles):
        step = low_tiles + no
        krow_ref[step] = sum(top_keys[no * quarters:(no + 1) * quarters])
        srow_ref[step] = sum(top_segs[no * quarters:(no + 1) * quarters])
        key = along_lanes(jnp.where(diag, jnp.broadcast_to(krow_ref[step], tile), 0.0))
        seg = along_lanes(jnp.where(diag, jnp.broadcast_to(srow_ref[step], tile), 0))
        keep(step, key < POS, key, seg)
    flags = jnp.max(jnp.where(iota((DEVS, LANES), 1) == FLAG, meta_all[:, 0, :], 0.0), axis=0, keepdims=True)
    flag_ref[...] = jnp.broadcast_to(jnp.max(flags, axis=1, keepdims=True), flag_ref.shape)

    def masks(step, carry):
        rows = pl.ds(pl.multiple_of(step * TALL, TALL), TALL)
        kcol = kcol_ref[rows]
        scol = scol_ref[rows]
        best = jnp.full((TALL, LANES), NEG, F32)
        for t in range(tiles):
            best = jnp.maximum(best, jnp.where((krow_ref[t] < kcol) & (srow_ref[t] != scol), krow_ref[t], NEG))
        bound = jnp.broadcast_to(jnp.max(best, axis=1, keepdims=True), best.shape)
        bcol_ref[rows] = bound
        for t in range(tiles):
            mask_ref[rows, t * LANES:(t + 1) * LANES] = hot((krow_ref[t] > bound) & (krow_ref[t] <= kcol))
        return carry

    lax.fori_loop(0, plan.need // TALL, masks, 0)

    krow = [krow_ref[t] for t in range(tiles)]
    srow = [srow_ref[t] for t in range(tiles)]

    def over(items, join, red):
        return red(functools.reduce(join, items), axis=1, keepdims=True)

    key_last = over([jnp.where(k < POS, k, NEG) for k in krow], jnp.maximum, jnp.max)
    key_first = over(krow, jnp.minimum, jnp.min)

    def pick(key):
        seg = over([jnp.where(k == key, s, 0) for k, s in zip(krow, srow)], jnp.add, jnp.sum)
        return seg, [(seg // HALF).astype(F32), (seg % HALF).astype(F32)]

    seg_last, last = pick(key_last)
    _, first = pick(key_first)
    cut = over([jnp.where((k < POS) & (s != seg_last), k, NEG) for k, s in zip(krow, srow)], jnp.maximum, jnp.max)
    tail_hot = jnp.concatenate([ones_where((k > cut) & (k < POS)) for k in krow], axis=1)
    tail_hot = jnp.broadcast_to(tail_hot, (BASE, plan.need)).astype(BF16)
    facts = jnp.zeros((1, LANES), F32)
    for no, val in enumerate(first + last + [ones_where(cut > NEG)]):
        facts = jnp.where(lane_one == no, val, facts)
    arrived(recv.at[most], row_sem)

    pile = LANES * 2
    piled = pile // quarters
    to, at = iota((pile, pile), 0), iota((pile, pile), 1)
    if more:
        widen = hot(to == fold(at, piled))
        for blk in range(plan.low // pile):
            full = dot(widen, recv[blk * pile:(blk + 1) * pile, cols:]).astype(BF16)
            for c in range(chunks):
                top_ref[blk * piled:(blk + 1) * piled, c * LANES:(c + 1) * LANES] = full[c * piled:(c + 1) * piled]

    def apply(mask):
        total = dot(mask[:, :plan.low], recv[:, :cols])
        return total + dot(mask[:, plan.low:], top_ref[...]) if more else total

    tail_msg[:, :cols] = apply(tail_hot)[:1]
    tail_msg[:, cols:] = facts
    for step in range(1, plan.ranges):
        remote(tail_msg, tail_all.at[my_range], tail_sem, (me + step * parts) & (DEVS - 1)).start()
    tail_all[my_range] = tail_msg[...]
    tails = tail_all.at[pl.ds(0, plan.ranges - 1)]
    arrived(tails, tail_sem)

    all_facts = tail_all[:, 0, cols:]
    fact_lane = iota((plan.ranges, LANES), 1)
    fact = [along_lanes(jnp.where(fact_lane == no, all_facts, 0.0)) for no in range(5)]
    range_no = iota((plan.ranges, 1), 0)
    before = range_no < my_range
    same_first = (fact[0] == first[0]) & (fact[1] == first[1])
    same_last = (fact[2] == first[0]) & (fact[3] == first[1])
    stop = before & ((fact[4] > 0.0) | jnp.logical_not(same_first))
    last_stop = jnp.max(jnp.where(stop, range_no, -1), axis=0, keepdims=True)
    linked = before & ((range_no > last_stop) | ((range_no == last_stop) & same_last))
    carry_in = along_sublanes(jnp.where(linked, tail_all[:, 0, :cols], 0.0))

    def finish(mask, bound):
        return (apply(mask) + jnp.where(bound[:, :1] == NEG, carry_in, 0.0)).astype(BF16)

    if more:
        narrow = hot(at == fold(to, piled))

        def top_sums(blk, carry):
            rows = pl.ds(pl.multiple_of(plan.low + blk * LANES, LANES), LANES)
            total = finish(mask_ref[rows], bcol_ref[rows])
            for no in range(LANES // piled):
                rows = total[no * piled:(no + 1) * piled]
                rows = jnp.concatenate([rows[:, c * LANES:(c + 1) * LANES] for c in range(chunks)], axis=0)
                start = pl.multiple_of((blk * (LANES // piled) + no) * pile, pile)
                sums_ref[pl.ds(start, pile), cols:] = dot(narrow, rows).astype(BF16)
            return carry

        lax.fori_loop(0, plan.top // LANES, top_sums, 0)

    def sums(blk, carry):
        devs = block_of_eight(me, blk)
        total = finish(jnp.concatenate([mask_ref[at16(dev)] for dev in devs], axis=0),
                       jnp.concatenate([bcol_ref[at16(dev)] for dev in devs], axis=0))
        for no, dev in enumerate(devs):
            sums_ref[at16(dev), :cols] = total[no * BASE:(no + 1) * BASE]
            send = remote(sums_ref.at[at16(dev)], ret.at[my_part, at16(my_range)], ret_sem, dev)
            pl.when(blk + no > 0)(send.start)
        return carry

    lax.fori_loop(0, DEVS // 8, sums, 0)
    ret[my_part, at16(my_range)] = sums_ref[at16(me)]
    arrived(recv.at[most], ret_sem)

    if more:
        piles = jnp.concatenate([ret[part, :, cols:] for part in range(parts)], axis=1)
        piles = dot(hot(iota(lines, 0) == fold(iota(lines, 1), plan.top_out)), piles).astype(BF16)
        for part in range(parts):
            for c in range(chunks):
                start = part * cols + c * LANES
                back_ref[:, start:start + LANES] = (
                    piles[c * plan.top_out:(c + 1) * plan.top_out, part * LANES:(part + 1) * LANES])
        hot_top = hot(top_col == iota((ROWS, plan.top_out), 1).astype(F32))
    hot_low = hot(low_col == iota((ROWS, plan.low_out), 1).astype(F32))
    for part in range(parts):
        here = slice(part * cols, (part + 1) * cols)
        rows = dot(hot_low, ret[part, :, :cols])
        if more:
            rows = rows + dot(hot_top, back_ref[:, here])
        out_ref[:, here] = rows.astype(BF16)

    for like in (samp_all.at[rest], meta_all.at[rest], recv.at[most], tails, recv.at[most]):
        left(like)


def run(plan, call_id, keys, segs, payload):
    vmem = pl.BlockSpec(memory_space=pltpu.VMEM)
    shapes = [
        ((1, LANES), F32),
        ((DEVS, 1, LANES), F32),
        ((plan.parts, plan.low_out, plan.line), BF16),
        ((plan.low, plan.line), BF16),
        ((plan.ranges, 1, LANES), F32),
        ((DEVS, 1, LANES), F32),
        ((plan.need, plan.need), BF16),
        ((plan.need, LANES), F32),
        ((plan.need, LANES), I32),
        ((plan.need, LANES), F32),
        ((plan.need // LANES, 1, LANES), F32),
        ((plan.need // LANES, 1, LANES), I32),
        ((1, plan.tail), F32),
        ((plan.ranges, 1, plan.tail), F32),
        ((max(plan.top, BASE), plan.cols), BF16),
        ((plan.low, plan.line), BF16),
        ((plan.parts, plan.low_out, plan.line), BF16),
        ((max(plan.top_out, BASE), WIDTH), BF16),
    ]
    return pl.pallas_call(
        functools.partial(kernel, plan),
        out_shape=(jax.ShapeDtypeStruct((ROWS, WIDTH), BF16), jax.ShapeDtypeStruct((8, LANES), F32)),
        in_specs=[vmem] * 3,
        out_specs=(vmem, vmem),
        scratch_shapes=[pltpu.VMEM(*shape) for shape in shapes] + [pltpu.SemaphoreType.DMA] * 6,
        compiler_params=pltpu.CompilerParams(collective_id=call_id, has_side_effects=True, vmem_limit_bytes=62 << 20),
    )(keys, segs, payload)


def solution(mesh):
    def per_device(sort_keys, seg_ids, payload):
        args = (sort_keys.reshape(1, ROWS), seg_ids.reshape(1, ROWS), payload)
        out, flag = run(NARROW, 0, *args)
        return lax.cond(flag[0, 0] > 0.0, lambda done: run(FULL, 1, *args)[0], lambda done: done, out)

    row_spec = P(('batch', 'group'))
    mat_spec = P(('batch', 'group'), None)
    return jax.shard_map(per_device, mesh=mesh, in_specs=(row_spec, row_spec, mat_spec),
                         out_specs=mat_spec, check_vma=False)
```

time: 646 us -> 127 us (0.20)
  the two profiles are of different devices: /device:TPU:1 before, /device:TPU:3 now
where the time goes in v2:
time: 127 us
  Pallas kernels  122 us (96%)
  local copies, waits for them, and re-layouts  4.36 us (3%)
    pallas_call x1, Pallas kernels, run(): pl.pallas_call(functools.partial(kernel, plan), out_shape=(jax.ShapeDtype...  122 us
    unnamed x5, local copies, waits for them, and re-layouts  3.17 us

profile of v2, /device:TPU:3, one launch (start us, length us, event | category | flops | bytes accessed | tf_op | source)
XLA Modules:
  0.0 127.1 jit_solution(2573178613134245864)
XLA Ops:
  0.0 0.0 copy-start.1
  0.0 0.0 copy-start
  0.0 121.8 %shard_map.39 = (bf16[512,2048]{1,0:T(8,128)(2,1)}, f32[8,128]{1,0:T(8,128)}) custom-call(f32[1,512]{1,0:T(1,128)} %bitcast.3, s32[1,512]{1,0:T(1,128)} %bitcast.5, bf16[512,2048]{1,0:T(8,128)(2,1)} %pay_ref.1), custom_call_target="tpu_custom_call" | custom-call | tf_op jit(solution)/shard_map/pallas_call | solution.py:389
  121.9 1.2 slice.3
  123.7 0.0 copy-done.1
  123.7 0.0 copy-done
  123.7 0.2 conditional.1
  123.9 3.2 %copy.9 = bf16[512,2048]{1,0:T(8,128)(2,1)} copy(bf16[512,2048]{1,0:T(8,128)(2,1)} %get-tuple-element.23) | data formatting | bytes 4194304
Async XLA Ops:
  0.0 123.7 %copy-start.1 = (s32[512]{0:T(512)S(1)}, s32[512]{0:T(512)}, u32[]{:S(2)}) copy-start(s32[512]{0:T(512)} %param.6) | copy-start | bytes 6148
  0.0 123.7 %copy-start = (f32[512]{0:T(512)S(1)}, f32[512]{0:T(512)}, u32[]{:S(2)}) copy-start(f32[512]{0:T(512)} %param.5) | copy-start | bytes 6148

commit v3 on v2

v3 whole, which is shorter than its diff:
```python
import functools

import jax
import jax.numpy as jnp
from jax import lax
from jax.experimental import pallas as pl
from jax.experimental.pallas import tpu as pltpu
from jax.sharding import PartitionSpec as P

F32 = jnp.float32
BF16 = jnp.bfloat16
I32 = jnp.int32
NEG = float('-inf')
POS = float('inf')
MESH = pl.DeviceIdType.MESH

DEVS = 128
ROWS = 512
WIDTH = 2048
LANES = 128
BASE = 16
MORE = 4
FLAG = LANES - 1
TALL = 32
EARLY = 32
RING = 4


class Plan:
    def __init__(self, parts, more, stride):
        self.parts, self.more, self.stride = parts, more, stride
        self.shift = parts.bit_length() - 1
        self.ranges = DEVS // parts
        self.per = ROWS // stride
        self.share = LANES // self.per
        self.cols = WIDTH // parts
        self.half = self.cols // 2
        self.chunks = self.cols // LANES
        self.full = BASE + more
        self.extra = LANES if more else 0
        self.long = self.half + self.extra
        self.low = DEVS * BASE
        self.top = DEVS * more
        self.need = self.low + self.top
        self.low_out = self.ranges * BASE
        self.top_out = self.ranges * more


NARROW = Plan(4, MORE, BASE)
FULL = Plan(2, 0, 4)


def iota(shape, dim):
    return lax.broadcasted_iota(I32, shape, dim)


def ones_where(hit):
    return jnp.where(hit, 1.0, 0.0)


def hot(hit):
    return ones_where(hit).astype(BF16)


def dot(left, right):
    return jnp.dot(left, right, preferred_element_type=F32)


def along_sublanes(vals):
    return jnp.sum(vals, axis=0, keepdims=True)


def along_lanes(vals):
    return jnp.sum(vals, axis=1, keepdims=True)


def fold(to, groups):
    return ((to & (BASE - 1)) >> 2) * groups + (to >> 4) * MORE + (to & (MORE - 1))


def fold_hot(size, groups):
    return hot(fold(iota((size, 1), 0), groups) == iota((1, size), 1))


def unfold_hot(size, groups):
    return hot(iota((size, 1), 0) == fold(iota((1, size), 1), groups))


def stack(rows, chunks):
    return jnp.concatenate([rows[:, c * LANES:(c + 1) * LANES] for c in range(chunks)], axis=0)


def place(me, step):
    core, x, y, z = me & 1, (me >> 1) & (RING - 1), (me >> 3) & (RING - 1), me >> 5
    return (core + step) & 1, ((x + step) & (RING - 1)) << 1, ((y + step) & (RING - 1)) << 3, ((z + step) & (RING - 1)) << 5


def other_devices(me):
    places = [place(me, step) for step in range(RING)]
    found = []
    for blk in range(DEVS // 8):
        for turn in range(RING):
            side = places[turn][1] + places[(turn + blk) % RING][2] + places[(turn + blk // RING) % RING][3]
            found += [side + places[flip][0] for flip in range(2)]
    return found[1:]


def kernel(plan, keys_ref, segs_ref, pay_hbm, out_ref, flag_ref, pay_ref, samp_msg, samp_all, fold_ref, packed0, packed1,
           recv0, recv1, meta_msg, meta_all, mask_ref, kcol_ref, scol_ref, bcol_ref, krow_ref, srow_ref, tail_msg0,
           tail_msg1, tail_all0, tail_all1, top_ref, acc_ref, top_done, sums0, sums1, ret0, ret1, back_ref, hot_low_ref,
           hot_top_ref, pay_sem, send_sem, samp_sem, meta_sem, row_sem0, row_sem1, tail_sem0, tail_sem1, ret_sem0,
           ret_sem1):
    parts, more, cols, half, chunks = plan.parts, plan.more, plan.cols, plan.half, plan.chunks
    me = lax.axis_index('group')
    my_range = me >> plan.shift
    my_part = me & (parts - 1)
    barrier = pltpu.get_barrier_semaphore()
    others = other_devices(me)
    rest = pl.ds(0, DEVS - 1)
    most = pl.ds(0, plan.low - BASE)

    def remote(src, dst, recv_sem, dev):
        return pltpu.make_async_remote_copy(src_ref=src, dst_ref=dst, send_sem=send_sem, recv_sem=recv_sem,
                                            device_id={'group': dev}, device_id_type=MESH)

    def arrived(like, sem):
        remote(like, like, sem, others[0]).wait_recv()

    def left(like):
        remote(like, like, ret_sem0, others[0]).wait_send()

    def at16(no):
        return pl.ds(pl.multiple_of(no * BASE, BASE), BASE)

    for dev in others:
        pl.semaphore_signal(barrier, inc=1, device_id={'group': dev}, device_id_type=MESH)
    fetch = pltpu.make_async_copy(pay_hbm, pay_ref, pay_sem)
    fetch.start()

    key_row = keys_ref[...]
    seg_row = segs_ref[...]
    square = (ROWS, ROWS)
    eye = iota(square, 0) == iota(square, 1)

    def to_col(row):
        return along_lanes(jnp.where(eye, jnp.broadcast_to(row, square), 0))

    def to_row(col):
        return along_sublanes(jnp.where(eye, jnp.broadcast_to(col, square), 0))

    key_col = to_col(key_row)
    rank_col = along_lanes(ones_where(key_row < key_col))
    wide = (ROWS, LANES)
    lane_one = iota((1, LANES), 1)
    chosen = ((lane_one - (me & (plan.share - 1)) * plan.per) * plan.stride).astype(F32)
    samp_msg[...] = along_sublanes(jnp.where(rank_col == chosen, jnp.broadcast_to(key_col, wide), 0.0))
    pl.semaphore_wait(barrier, DEVS - 1)

    for dev in others:
        remote(samp_msg, samp_all.at[me], samp_sem, dev).start()
    samp_all[me] = samp_msg[...]
    if more:
        fold_ref[...] = fold_hot(plan.low_out, plan.top_out)
    seg_col = to_col(seg_row)
    arrived(samp_all.at[rest], samp_sem)

    tile = (LANES, LANES)
    counts = []
    for part in range(ROWS // LANES):
        kblk = jnp.broadcast_to(key_col[part * LANES:(part + 1) * LANES], tile)

        def count(step, acc, kblk=kblk):
            for sub in range(8):
                row = (step * 8 + sub) * plan.share
                acc = acc + ones_where(sum(samp_all[row + no] for no in range(plan.share)) <= kblk)
            return acc

        counts.append(along_lanes(lax.fori_loop(0, plan.per // 8, count, jnp.zeros(tile, F32))))
    seen_col = jnp.concatenate(counts, axis=0)
    per_range = DEVS * plan.per // plan.ranges
    range_col = jnp.maximum(jnp.floor((seen_col - (DEVS // 2 + 1)) * (1.0 / per_range)), 0.0)
    range_row = to_row(range_col)
    slot_col = rank_col - along_lanes(ones_where(range_row < range_col))
    low_col = jnp.where(slot_col < BASE, range_col * BASE + slot_col, -1.0)
    low_row = to_row(low_col)
    top_col = jnp.where((slot_col >= BASE) & (slot_col < plan.full), range_col * more + (slot_col - BASE), -1.0)
    spill = ones_where(jnp.max(slot_col, axis=0, keepdims=True) >= plan.full)

    hot_low = hot(low_row == iota((plan.low_out, 1), 0).astype(F32))
    if more:
        hot_top = hot(to_row(top_col) == iota((plan.top_out, 1), 0).astype(F32))
    fetch.wait()
    piles = []
    for part in range(parts):
        start = part * cols
        packed0[part, :, :half] = dot(hot_low, pay_ref[:, start:start + half]).astype(BF16)
        if more:
            piles.append(stack(dot(hot_top, pay_ref[:, start:start + cols]).astype(BF16), chunks))
    if more:
        folded = dot(fold_ref[...], jnp.concatenate(piles, axis=1)).astype(BF16)
        for part in range(parts):
            packed0[part, :, half:] = folded[:, part * LANES:(part + 1) * LANES]

    def send_rows(devs, src, dst, sem):
        for dev in devs:
            remote(src.at[dev & (parts - 1), at16(dev >> plan.shift)], dst.at[at16(me)], sem, dev).start()

    send_rows(others[:EARLY], packed0, recv0, row_sem0)

    lane_val = lane_one // plan.full
    lane_slot = (lane_one % plan.full).astype(F32)
    vals = jnp.where(lane_val == 0, key_col, 1.0)
    vals = jnp.where(lane_val == 1, (seg_col >> 16).astype(F32), vals)
    vals = jnp.where(lane_val == 2, (seg_col & 65535).astype(F32), vals)
    vals = jnp.where((lane_slot == slot_col) & (lane_val < 4), vals, 0.0)
    range_b = jnp.broadcast_to(range_col, wide)
    for dst in range(plan.ranges):
        meta = along_sublanes(jnp.where(range_b == float(dst), vals, 0.0))
        meta_msg[dst] = jnp.where(lane_one == FLAG, spill, meta)
    for dev in others:
        remote(meta_msg.at[dev >> plan.shift], meta_all.at[me], meta_sem, dev).start()
    meta_all[me] = meta_msg[my_range]
    send_rows(others[EARLY:], packed0, recv0, row_sem0)

    for part in range(parts):
        start = part * cols + half
        packed1[part] = dot(hot_low, pay_ref[:, start:start + half]).astype(BF16)
    send_rows(others, packed1, recv1, row_sem1)
    recv0[at16(me)] = packed0[my_part, at16(my_range)]
    recv1[at16(me)] = packed1[my_part, at16(my_range)]
    arrived(meta_all.at[rest], meta_sem)

    low_tiles = plan.low // LANES
    tiles = plan.need // LANES
    each = LANES // BASE
    quarters = BASE // MORE
    sub = iota((LANES, 1), 0)
    diag = sub == lane_one

    def read_slots(got, slot):
        found = [along_lanes(jnp.where(lane_one == slot + no * plan.full, got, 0.0)) for no in range(4)]
        seg = (found[1].astype(I32) << 16) + found[2].astype(I32)
        return found[3] > 0.0, found[0], seg

    def keep(step, live, key, seg):
        rows = pl.ds(step * LANES, LANES)
        kcol_ref[rows] = jnp.broadcast_to(jnp.where(live, key, NEG), tile)
        scol_ref[rows] = jnp.broadcast_to(seg, tile)

    def to_lanes(spot, live, key, seg):
        return along_sublanes(jnp.where(spot, jnp.where(live, key, POS), 0.0)), along_sublanes(jnp.where(spot, seg, 0))

    top_keys, top_segs = [], []
    for step in range(low_tiles):
        got = meta_all[step * each:(step + 1) * each]
        got = jnp.broadcast_to(got, (each, BASE, LANES)).reshape(tile)
        slots = read_slots(got, sub & (BASE - 1))
        keep(step, *slots)
        krow_ref[step], srow_ref[step] = to_lanes(diag, *slots)
        if more:
            first = (step % quarters) * (LANES // quarters)
            spot = (lane_one == first + (sub >> 4) * MORE + (sub & (MORE - 1))) & ((sub & (BASE - 1)) < MORE)
            key, seg = to_lanes(spot, *read_slots(got, BASE + (sub & (MORE - 1))))
            top_keys.append(key)
            top_segs.append(seg)
    for no in range(tiles - low_tiles):
        step = low_tiles + no
        krow_ref[step] = sum(top_keys[no * quarters:(no + 1) * quarters])
        srow_ref[step] = sum(top_segs[no * quarters:(no + 1) * quarters])
        key = along_lanes(jnp.where(diag, jnp.broadcast_to(krow_ref[step], tile), 0.0))
        seg = along_lanes(jnp.where(diag, jnp.broadcast_to(srow_ref[step], tile), 0))
        keep(step, key < POS, key, seg)
    flags = jnp.max(jnp.where(lane_one == FLAG, meta_all[:, 0, :], 0.0), axis=0, keepdims=True)
    flag_ref[...] = jnp.broadcast_to(jnp.max(flags, axis=1, keepdims=True), flag_ref.shape)

    def masks(step, carry):
        rows = pl.ds(pl.multiple_of(step * TALL, TALL), TALL)
        kcol = kcol_ref[rows]
        scol = scol_ref[rows]
        best = jnp.full((TALL, LANES), NEG, F32)
        for t in range(tiles):
            best = jnp.maximum(best, jnp.where((krow_ref[t] < kcol) & (srow_ref[t] != scol), krow_ref[t], NEG))
        bound = jnp.broadcast_to(jnp.max(best, axis=1, keepdims=True), best.shape)
        bcol_ref[rows] = bound
        for t in range(tiles):
            mask_ref[rows, t * LANES:(t + 1) * LANES] = hot((krow_ref[t] > bound) & (krow_ref[t] <= kcol))
        return carry

    lax.fori_loop(0, plan.need // TALL, masks, 0)

    krow = [krow_ref[t] for t in range(tiles)]
    srow = [srow_ref[t] for t in range(tiles)]

    def over(items, join, red):
        return red(functools.reduce(join, items), axis=1, keepdims=True)

    key_last = over([jnp.where(k < POS, k, NEG) for k in krow], jnp.maximum, jnp.max)
    key_first = over(krow, jnp.minimum, jnp.min)

    def pick(key):
        seg = over([jnp.where(k == key, s, 0) for k, s in zip(krow, srow)], jnp.add, jnp.sum)
        return seg, [(seg >> 16).astype(F32), (seg & 65535).astype(F32)]

    seg_last, last = pick(key_last)
    _, first = pick(key_first)
    cut = over([jnp.where((k < POS) & (s != seg_last), k, NEG) for k, s in zip(krow, srow)], jnp.maximum, jnp.max)
    tail_hot = jnp.concatenate([ones_where((k > cut) & (k < POS)) for k in krow], axis=1)
    tail_hot = jnp.broadcast_to(tail_hot, (BASE, plan.need)).astype(BF16)
    facts = jnp.zeros((1, LANES), F32)
    for no, val in enumerate(first + last + [ones_where(cut > NEG)]):
        facts = jnp.where(lane_one == no, val, facts)

    hot_low_ref[...] = hot(low_col == iota((1, plan.low_out), 1).astype(F32))
    if more:
        fold_ref[...] = unfold_hot(plan.low_out, plan.top_out)
        hot_top_ref[...] = hot(top_col == iota((1, plan.top_out), 1).astype(F32))

    def apply(mask, recv, no):
        total = dot(mask[:, :plan.low], recv[:, :half])
        return total + dot(mask[:, plan.low:], top_ref[:, no * half:(no + 1) * half]) if more else total

    def send_tail(msg, dst, sem):
        for step in range(1, plan.ranges):
            remote(msg, dst.at[my_range], sem, (me + step * parts) & (DEVS - 1)).start()
        dst[my_range] = msg[...]

    big = 256

    def products(recv, no):
        def step(blk, carry):
            rows = pl.ds(pl.multiple_of(blk * big, big), big)
            acc_ref[rows] = apply(mask_ref[rows], recv, no)
            return carry

        lax.fori_loop(0, plan.need // big, step, 0)

    arrived(recv0.at[most], row_sem0)
    piled = big // quarters
    if more:
        widen = unfold_hot(big, piled)
        for blk in range(plan.low // big):
            full = dot(widen, recv0[blk * big:(blk + 1) * big, half:]).astype(BF16)
            for c in range(chunks):
                top_ref[blk * piled:(blk + 1) * piled, c * LANES:(c + 1) * LANES] = full[c * piled:(c + 1) * piled]
    tail_msg0[:, :half] = apply(tail_hot, recv0, 0)[:1]
    tail_msg0[:, half:] = facts
    send_tail(tail_msg0, tail_all0, tail_sem0)
    products(recv0, 0)
    arrived(recv1.at[most], row_sem1)
    tail_msg1[...] = apply(tail_hot, recv1, 1)[:1]
    send_tail(tail_msg1, tail_all1, tail_sem1)
    tails0 = tail_all0.at[pl.ds(0, plan.ranges - 1)]
    tails1 = tail_all1.at[pl.ds(0, plan.ranges - 1)]
    arrived(tails0, tail_sem0)

    fact = [along_lanes(jnp.where(lane_one == no, tail_all0[:, 0, half:], 0.0)) for no in range(5)]
    range_no = iota((plan.ranges, 1), 0)
    before = range_no < my_range
    same_first = (fact[0] == first[0]) & (fact[1] == first[1])
    same_last = (fact[2] == first[0]) & (fact[3] == first[1])
    stop = before & ((fact[4] > 0.0) | jnp.logical_not(same_first))
    last_stop = jnp.max(jnp.where(stop, range_no, -1), axis=0, keepdims=True)
    linked = before & ((range_no > last_stop) | ((range_no == last_stop) & same_last))

    def finish(tails, no, sums):
        carry_in = along_sublanes(jnp.where(linked, tails[:, 0, :half], 0.0))

        def closed(rows):
            return (acc_ref[rows] + jnp.where(bcol_ref[rows][:, :1] == NEG, carry_in, 0.0)).astype(BF16)

        def step(blk, carry):
            rows = pl.ds(pl.multiple_of(blk * big, big), big)
            sums[rows, :half] = closed(rows)
            return carry

        lax.fori_loop(0, plan.low // big, step, 0)
        if more:
            top_done[:, no * half:(no + 1) * half] = closed(pl.ds(plan.low, plan.top))

    def send_back(src, dst, sem):
        for dev in others:
            remote(src.at[at16(dev)], dst.at[my_part, at16(my_range)], sem, dev).start()
        dst[my_part, at16(my_range)] = src[at16(me)]

    finish(tail_all0, 0, sums0)
    send_back(sums0, ret0, ret_sem0)

    products(recv1, 1)
    arrived(tails1, tail_sem1)
    finish(tail_all1, 1, sums1)
    if more:
        narrow = fold_hot(big, piled)
        for blk in range(plan.top // piled):
            pile = stack(top_done[blk * piled:(blk + 1) * piled], chunks)
            sums1[blk * big:(blk + 1) * big, half:] = dot(narrow, pile).astype(BF16)
    send_back(sums1, ret1, ret_sem1)

    arrived(recv1.at[most], ret_sem0)
    if not more:
        for part in range(parts):
            start = part * cols
            out_ref[:, start:start + half] = dot(hot_low_ref[...], ret0[part]).astype(BF16)
    else:
        for part in range(parts):
            back_ref[:, part * half:(part + 1) * half] = dot(hot_low_ref[...], ret0[part])
    arrived(recv0.at[most], ret_sem1)
    if more:
        piles = jnp.concatenate([ret1[part, :, half:] for part in range(parts)], axis=1)
        piles = dot(fold_ref[...], piles).astype(BF16)
    for part in range(parts):
        start = part * cols
        rows = dot(hot_low_ref[...], ret1[part, :, :half])
        if more:
            top_rows = jnp.concatenate([piles[c * plan.top_out:(c + 1) * plan.top_out, part * LANES:(part + 1) * LANES]
                                        for c in range(chunks)], axis=1)
            top_rows = dot(hot_top_ref[...], top_rows)
            rows = rows + top_rows[:, half:]
            out_ref[:, start:start + half] = (back_ref[:, part * half:(part + 1) * half] + top_rows[:, :half]).astype(BF16)
        out_ref[:, start + half:start + cols] = rows.astype(BF16)

    for like in (samp_all.at[rest], meta_all.at[rest], recv0.at[most], recv1.at[most], tails0, tails1, recv0.at[most],
                 recv1.at[most]):
        left(like)


def run(plan, call_id, keys, segs, payload):
    vmem = pl.BlockSpec(memory_space=pltpu.VMEM)
    shapes = [
        ((ROWS, WIDTH), BF16),
        ((1, LANES), F32),
        ((DEVS, 1, LANES), F32),
        ((plan.low_out, plan.low_out) if plan.more else (BASE, LANES), BF16),
        ((plan.parts, plan.low_out, plan.long), BF16),
        ((plan.parts, plan.low_out, plan.half), BF16),
        ((plan.low, plan.long), BF16),
        ((plan.low, plan.half), BF16),
        ((plan.ranges, 1, LANES), F32),
        ((DEVS, 1, LANES), F32),
        ((plan.need, plan.need), BF16),
        ((plan.need, LANES), F32),
        ((plan.need, LANES), I32),
        ((plan.need, LANES), F32),
        ((plan.need // LANES, 1, LANES), F32),
        ((plan.need // LANES, 1, LANES), I32),
        ((1, plan.half + LANES), F32),
        ((1, plan.half), F32),
        ((plan.ranges, 1, plan.half + LANES), F32),
        ((plan.ranges, 1, plan.half), F32),
        ((max(plan.top, BASE), plan.cols), BF16),
        ((plan.need, plan.half), F32),
        ((max(plan.top, BASE), plan.cols), BF16),
        ((plan.low, plan.half), BF16),
        ((plan.low, plan.long), BF16),
        ((plan.parts, plan.low_out, plan.half), BF16),
        ((plan.parts, plan.low_out, plan.long), BF16),
        ((ROWS, WIDTH // 2) if plan.more else (8, LANES), F32),
        ((ROWS, plan.low_out), BF16),
        ((ROWS, max(plan.top_out, LANES)), BF16),
    ]
    return pl.pallas_call(
        functools.partial(kernel, plan),
        out_shape=(jax.ShapeDtypeStruct((ROWS, WIDTH), BF16), jax.ShapeDtypeStruct((8, LANES), F32)),
        in_specs=[vmem, vmem, pl.BlockSpec(memory_space=pl.ANY)],
        out_specs=(vmem, vmem),
        scratch_shapes=[pltpu.VMEM(*shape) for shape in shapes] + [pltpu.SemaphoreType.DMA] * 10,
        compiler_params=pltpu.CompilerParams(collective_id=call_id, has_side_effects=True, vmem_limit_bytes=62 << 20),
    )(keys, segs, payload)


def solution(mesh):
    def per_device(sort_keys, seg_ids, payload):
        args = (sort_keys.reshape(1, ROWS), seg_ids.reshape(1, ROWS), payload)
        out, flag = run(NARROW, 0, *args)
        return lax.cond(flag[0, 0] > 0.0, lambda done: run(FULL, 1, *args)[0], lambda done: done, out)

    row_spec = P(('batch', 'group'))
    mat_spec = P(('batch', 'group'), None)
    return jax.shard_map(per_device, mesh=mesh, in_specs=(row_spec, row_spec, mat_spec),
                         out_specs=mat_spec, check_vma=False)
```

time: 127 us -> 109 us (0.86)
  the two profiles are of different devices: /device:TPU:3 before, /device:TPU:1 now
where the time goes in v3:
time: 109 us
  Pallas kernels  104 us (95%)
  local copies, waits for them, and re-layouts  4.36 us (4%)
    pallas_call x1, Pallas kernels, run(): pl.pallas_call(functools.partial(kernel, plan), out_shape=(jax.ShapeDtype...  104 us
    unnamed x5, local copies, waits for them, and re-layouts  3.17 us

profile of v3, /device:TPU:1, one launch (start us, length us, event | category | flops | bytes accessed | tf_op | source)
XLA Modules:
  0.0 108.9 jit_solution(10065995486297267800)
XLA Ops:
  0.0 0.0 copy-start.1
  0.0 0.0 copy-start
  0.0 103.6 %shard_map.39 = (bf16[512,2048]{1,0:T(8,128)(2,1)}, f32[8,128]{1,0:T(8,128)}) custom-call(f32[1,512]{1,0:T(1,128)} %bitcast.3, s32[1,512]{1,0:T(1,128)} %bitcast.5, bf16[512,2048]{1,0:T(8,128)(2,1)} %pay_hbm.1), custom_call_target="tpu_custom_call" | custom-call | tf_op jit(solution)/shard_map/pallas_call | solution.py:460
  103.6 1.2 %slice.3 = f32[1,1]{1,0:T(1,128)} slice(f32[8,128]{1,0:T(8,128)} %get-tuple-element.21), slice={[0:1], [0:1]} | slice | bytes 8 | tf_op jit(solution)/shard_map/slice | solution.py:474
  105.5 0.0 copy-done.1
  105.5 0.0 copy-done
  105.5 0.2 conditional.1
  105.7 3.2 %copy.9 = bf16[512,2048]{1,0:T(8,128)(2,1)} copy(bf16[512,2048]{1,0:T(8,128)(2,1)} %get-tuple-element.23) | data formatting | bytes 4194304
Async XLA Ops:
  0.0 105.5 %copy-start.1 = (s32[512]{0:T(512)S(1)}, s32[512]{0:T(512)}, u32[]{:S(2)}) copy-start(s32[512]{0:T(512)} %param.6) | copy-start | bytes 6148
  0.0 105.5 %copy-start = (f32[512]{0:T(512)S(1)}, f32[512]{0:T(512)}, u32[]{:S(2)}) copy-start(f32[512]{0:T(512)} %param.5) | copy-start | bytes 6148

commit v4 on v3

--- a/solution.py
+++ b/solution.py
@@ -98,11 +98,22 @@
 def other_devices(me):
     places = [place(me, step) for step in range(RING)]
     found = []
-    for blk in range(DEVS // 8):
-        for turn in range(RING):
-            side = places[turn][1] + places[(turn + blk) % RING][2] + places[(turn + blk // RING) % RING][3]
-            found += [side + places[flip][0] for flip in range(2)]
-    return found[1:]
+
+    def add(along_x, along_y, along_z, flip):
+        found.append(places[along_z % RING][3] + places[along_y % RING][2] + places[along_x][1] + places[flip][0])
+
+    for near in (True, False):
+        for flip in range(2):
+            for along_z in range(RING):
+                for along_y in range(RING):
+                    if near:
+                        add(1, along_y, along_z, flip)
+                        add(3, along_y + 2, along_z + 2, flip)
+                    else:
+                        add(2, along_y + 2, along_z + 2, flip)
+                        if along_y or along_z or flip:
+                            add(0, along_y, along_z, flip)
+    return found
 
 
 def kernel(plan, keys_ref, segs_ref, pay_hbm, out_ref, flag_ref, pay_ref, samp_msg, samp_all, fold_ref, packed0, packed1,
@@ -271,7 +282,7 @@
         seg = along_lanes(jnp.where(diag, jnp.broadcast_to(srow_ref[step], tile), 0))
         keep(step, key < POS, key, seg)
     flags = jnp.max(jnp.where(lane_one == FLAG, meta_all[:, 0, :], 0.0), axis=0, keepdims=True)
-    flag_ref[...] = jnp.broadcast_to(jnp.max(flags, axis=1, keepdims=True), flag_ref.shape)
+    flag_ref[0, 0] = jnp.max(flags)
 
     def masks(step, carry):
         rows = pl.ds(pl.multiple_of(step * TALL, TALL), TALL)
@@ -459,19 +470,29 @@
     ]
     return pl.pallas_call(
         functools.partial(kernel, plan),
-        out_shape=(jax.ShapeDtypeStruct((ROWS, WIDTH), BF16), jax.ShapeDtypeStruct((8, LANES), F32)),
+        out_shape=(jax.ShapeDtypeStruct((ROWS, WIDTH), BF16), jax.ShapeDtypeStruct((1, 1), F32)),
         in_specs=[vmem, vmem, pl.BlockSpec(memory_space=pl.ANY)],
-        out_specs=(vmem, vmem),
+        out_specs=(vmem, pl.BlockSpec(memory_space=pltpu.SMEM)),
         scratch_shapes=[pltpu.VMEM(*shape) for shape in shapes] + [pltpu.SemaphoreType.DMA] * 10,
         compiler_params=pltpu.CompilerParams(collective_id=call_id, has_side_effects=True, vmem_limit_bytes=62 << 20),
     )(keys, segs, payload)
+
+
+def settle_kernel(src_ref, dst_ref):
+    dst_ref[...] = src_ref[...]
+
+
+def settle(done):
+    block = pl.BlockSpec((ROWS // 4, WIDTH), lambda step: (step, 0))
+    return pl.pallas_call(settle_kernel, out_shape=jax.ShapeDtypeStruct((ROWS, WIDTH), BF16), grid=(4,),
+                          in_specs=[block], out_specs=block)(done)
 
 
 def solution(mesh):
     def per_device(sort_keys, seg_ids, payload):
         args = (sort_keys.reshape(1, ROWS), seg_ids.reshape(1, ROWS), payload)
         out, flag = run(NARROW, 0, *args)
-        return lax.cond(flag[0, 0] > 0.0, lambda done: run(FULL, 1, *args)[0], lambda done: done, out)
+        return settle(lax.cond(flag[0, 0] > 0.0, lambda done: run(FULL, 1, *args)[0], lambda done: done, out))
 
     row_spec = P(('batch', 'group'))
     mat_spec = P(('batch', 'group'), None)

time: 109 us -> 103 us (0.945); the launches traced: 109 us -> 101 us
  local copies, waits for them, and re-layouts: 4.36 us -> 0.01 us
  Pallas kernels: 104 us -> 100 us
    pallas_call x1, Pallas kernels: 104 us -> 96.7 us  [run(): pl.pallas_call(functools.partial(kernel, plan), out_shape=(jax.ShapeDtype...]
    pallas_call x0 -> x1, Pallas kernels: none -> 3.78 us  [settle(): pl.pallas_call(settle_kernel, out_shape=jax.ShapeDtypeStruct((ROWS, WIDTH...]
    unnamed x5 -> x4, local copies, waits for them, and re-layouts: 3.17 us -> 0.01 us
    slice x1 -> x0, local copies, waits for them, and re-layouts: 1.2 us -> none  [per_device(): flag[0, 0] > 0.0]
where the time goes in v4:
time: 103 us; the launch traced here: 101 us
  Pallas kernels  100 us (97%)
    pallas_call x1, Pallas kernels, run(): pl.pallas_call(functools.partial(kernel, plan), out_shape=(jax.ShapeDtype...  96.7 us
    pallas_call x1, Pallas kernels, settle(): pl.pallas_call(settle_kernel, out_shape=jax.ShapeDtypeStruct((ROWS, WIDTH...  3.78 us

profile of v4, /device:TPU:1, one launch (start us, length us, event | category | flops | bytes accessed | tf_op | source)
XLA Modules:
  0.0 101.3 jit_solution(8922424114472778463)
XLA Ops:
  0.0 0.0 copy-start.1
  0.0 0.0 copy-start
  0.0 96.7 %shard_map.37 = (bf16[512,2048]{1,0:T(8,128)(2,1)}, f32[1,1]{1,0:T(1,128)}) custom-call(f32[1,512]{1,0:T(1,128)} %bitcast.3, s32[1,512]{1,0:T(1,128)} %bitcast.5, bf16[512,2048]{1,0:T(8,128)(2,1)} %pay_hbm.1), custom_call_target="tpu_custom_call" | custom-call | tf_op jit(solution)/shard_map/pallas_call | solution.py:471
  97.3 0.0 copy-done.1
  97.3 0.0 copy-done
  97.3 0.2 conditional.1
  97.5 3.8 %shard_map.38 = bf16[512,2048]{1,0:T(8,128)(2,1)} custom-call(bf16[512,2048]{1,0:T(8,128)(2,1)} %get-tuple-element.23.src_ref), custom_call_target="tpu_custom_call" | custom-call | tf_op jit(solution)/shard_map/pallas_call | solution.py:487
Async XLA Ops:
  0.0 97.3 %copy-start.1 = (s32[512]{0:T(512)S(1)}, s32[512]{0:T(512)}, u32[]{:S(2)}) copy-start(s32[512]{0:T(512)} %param.6) | copy-start | bytes 6148
  0.0 97.3 %copy-start = (f32[512]{0:T(512)S(1)}, f32[512]{0:T(512)}, u32[]{:S(2)}) copy-start(f32[512]{0:T(512)} %param.5) | copy-start | bytes 6148

commit v5 on v4

--- a/solution.py
+++ b/solution.py
@@ -21,8 +21,7 @@
 BASE = 16
 MORE = 4
 FLAG = LANES - 1
-TALL = 32
-EARLY = 32
+TALL = 128
 RING = 4
 
 
@@ -97,13 +96,14 @@
 
 def other_devices(me):
     places = [place(me, step) for step in range(RING)]
-    found = []
+    found, starts = [], []
 
     def add(along_x, along_y, along_z, flip):
         found.append(places[along_z % RING][3] + places[along_y % RING][2] + places[along_x][1] + places[flip][0])
 
     for near in (True, False):
         for flip in range(2):
+            starts.append(len(found))
             for along_z in range(RING):
                 for along_y in range(RING):
                     if near:
@@ -113,20 +113,20 @@
                         add(2, along_y + 2, along_z + 2, flip)
                         if along_y or along_z or flip:
                             add(0, along_y, along_z, flip)
-    return found
-
-
-def kernel(plan, keys_ref, segs_ref, pay_hbm, out_ref, flag_ref, pay_ref, samp_msg, samp_all, fold_ref, packed0, packed1,
+    return found, starts
+
+
+def kernel(plan, keys_ref, segs_ref, pay_hbm, out_hbm, flag_ref, pay_ref, samp_msg, samp_all, fold_ref, packed0, packed1,
            recv0, recv1, meta_msg, meta_all, mask_ref, kcol_ref, scol_ref, bcol_ref, krow_ref, srow_ref, tail_msg0,
            tail_msg1, tail_all0, tail_all1, top_ref, acc_ref, top_done, sums0, sums1, ret0, ret1, back_ref, hot_low_ref,
            hot_top_ref, pay_sem, send_sem, samp_sem, meta_sem, row_sem0, row_sem1, tail_sem0, tail_sem1, ret_sem0,
-           ret_sem1):
+           ret_sem1, out_sem):
     parts, more, cols, half, chunks = plan.parts, plan.more, plan.cols, plan.half, plan.chunks
     me = lax.axis_index('group')
     my_range = me >> plan.shift
     my_part = me & (parts - 1)
     barrier = pltpu.get_barrier_semaphore()
-    others = other_devices(me)
+    others, starts = other_devices(me)
     rest = pl.ds(0, DEVS - 1)
     most = pl.ds(0, plan.low - BASE)
 
@@ -201,42 +201,50 @@
     if more:
         hot_top = hot(to_row(top_col) == iota((plan.top_out, 1), 0).astype(F32))
     fetch.wait()
-    piles = []
-    for part in range(parts):
-        start = part * cols
-        packed0[part, :, :half] = dot(hot_low, pay_ref[:, start:start + half]).astype(BF16)
+    turns = [others[no] & (parts - 1) for no in starts]
+
+    def pack(part, dst, first):
+        start = part * cols + first
+        rows = pay_ref[:, pl.ds(pl.multiple_of(start, half), half)]
+        dst[part, :, :half] = dot(hot_low, rows).astype(BF16)
+
+    def pack_top(part):
+        rows = dot(hot_top, pay_ref[:, pl.ds(pl.multiple_of(part * cols, cols), cols)]).astype(BF16)
+        packed0[part, :, half:] = dot(fold_ref[...], stack(rows, chunks)).astype(BF16)
+
+    def pack_first(part):
+        pack(part, packed0, 0)
         if more:
-            piles.append(stack(dot(hot_top, pay_ref[:, start:start + cols]).astype(BF16), chunks))
-    if more:
-        folded = dot(fold_ref[...], jnp.concatenate(piles, axis=1)).astype(BF16)
-        for part in range(parts):
-            packed0[part, :, half:] = folded[:, part * LANES:(part + 1) * LANES]
-
-    def send_rows(devs, src, dst, sem):
-        for dev in devs:
+            pack_top(part)
+
+    def send_rows(no, src, dst, sem):
+        for dev in others[starts[no]:(starts + [DEVS - 1])[no + 1]]:
             remote(src.at[dev & (parts - 1), at16(dev >> plan.shift)], dst.at[at16(me)], sem, dev).start()
 
-    send_rows(others[:EARLY], packed0, recv0, row_sem0)
+    pack_first(turns[0])
+    send_rows(0, packed0, recv0, row_sem0)
 
     lane_val = lane_one // plan.full
     lane_slot = (lane_one % plan.full).astype(F32)
-    vals = jnp.where(lane_val == 0, key_col, 1.0)
+    vals = jnp.where(lane_val == 0, key_col, (seg_col & 65535).astype(F32))
     vals = jnp.where(lane_val == 1, (seg_col >> 16).astype(F32), vals)
-    vals = jnp.where(lane_val == 2, (seg_col & 65535).astype(F32), vals)
-    vals = jnp.where((lane_slot == slot_col) & (lane_val < 4), vals, 0.0)
+    vals = jnp.where((lane_slot == slot_col) & (lane_val < 3), vals, POS)
     range_b = jnp.broadcast_to(range_col, wide)
     for dst in range(plan.ranges):
-        meta = along_sublanes(jnp.where(range_b == float(dst), vals, 0.0))
+        meta = jnp.min(jnp.where(range_b == float(dst), vals, POS), axis=0, keepdims=True)
         meta_msg[dst] = jnp.where(lane_one == FLAG, spill, meta)
     for dev in others:
         remote(meta_msg.at[dev >> plan.shift], meta_all.at[me], meta_sem, dev).start()
     meta_all[me] = meta_msg[my_range]
-    send_rows(others[EARLY:], packed0, recv0, row_sem0)
-
-    for part in range(parts):
-        start = part * cols + half
-        packed1[part] = dot(hot_low, pay_ref[:, start:start + half]).astype(BF16)
-    send_rows(others, packed1, recv1, row_sem1)
+    for no in range(1, len(turns)):
+        if no < parts:
+            pack_first(turns[no])
+        send_rows(no, packed0, recv0, row_sem0)
+
+    for no in range(len(turns)):
+        if no < parts:
+            pack(turns[no], packed1, half)
+        send_rows(no, packed1, recv1, row_sem1)
     recv0[at16(me)] = packed0[my_part, at16(my_range)]
     recv1[at16(me)] = packed1[my_part, at16(my_range)]
     arrived(meta_all.at[rest], meta_sem)
@@ -249,35 +257,37 @@
     diag = sub == lane_one
 
     def read_slots(got, slot):
-        found = [along_lanes(jnp.where(lane_one == slot + no * plan.full, got, 0.0)) for no in range(4)]
-        seg = (found[1].astype(I32) << 16) + found[2].astype(I32)
-        return found[3] > 0.0, found[0], seg
+        found = [along_lanes(jnp.where(lane_one == slot + no * plan.full, got, 0.0)) for no in range(3)]
+        live = found[0] < POS
+        high, low = [jnp.where(live, val, 0.0).astype(I32) for val in found[1:]]
+        return live, found[0], (high << 16) + low
 
     def keep(step, live, key, seg):
         rows = pl.ds(step * LANES, LANES)
         kcol_ref[rows] = jnp.broadcast_to(jnp.where(live, key, NEG), tile)
         scol_ref[rows] = jnp.broadcast_to(seg, tile)
 
-    def to_lanes(spot, live, key, seg):
-        return along_sublanes(jnp.where(spot, jnp.where(live, key, POS), 0.0)), along_sublanes(jnp.where(spot, seg, 0))
-
-    top_keys, top_segs = [], []
+    def to_lanes(step, spot, key, seg):
+        krow_ref[step] = along_sublanes(jnp.where(spot, key, 0.0))
+        srow_ref[step] = along_sublanes(jnp.where(spot, seg, 0))
+
+    mixed = []
     for step in range(low_tiles):
         got = meta_all[step * each:(step + 1) * each]
         got = jnp.broadcast_to(got, (each, BASE, LANES)).reshape(tile)
-        slots = read_slots(got, sub & (BASE - 1))
-        keep(step, *slots)
-        krow_ref[step], srow_ref[step] = to_lanes(diag, *slots)
+        live, key, seg = read_slots(got, sub & (BASE - 1))
+        keep(step, live, key, seg)
+        to_lanes(step, diag, key, seg)
         if more:
-            first = (step % quarters) * (LANES // quarters)
-            spot = (lane_one == first + (sub >> 4) * MORE + (sub & (MORE - 1))) & ((sub & (BASE - 1)) < MORE)
-            key, seg = to_lanes(spot, *read_slots(got, BASE + (sub & (MORE - 1))))
-            top_keys.append(key)
-            top_segs.append(seg)
-    for no in range(tiles - low_tiles):
+            turn = step % quarters
+            merged = jnp.where(((sub & (BASE - 1)) >> 2) == turn, got, merged if turn else 0.0)
+            if turn == quarters - 1:
+                mixed.append(merged)
+    for no, merged in enumerate(mixed):
         step = low_tiles + no
-        krow_ref[step] = sum(top_keys[no * quarters:(no + 1) * quarters])
-        srow_ref[step] = sum(top_segs[no * quarters:(no + 1) * quarters])
+        _, key, seg = read_slots(merged, BASE + (sub & (MORE - 1)))
+        spot = lane_one == (((sub & (BASE - 1)) >> 2) * each + (sub >> 4)) * MORE + (sub & (MORE - 1))
+        to_lanes(step, spot, key, seg)
         key = along_lanes(jnp.where(diag, jnp.broadcast_to(krow_ref[step], tile), 0.0))
         seg = along_lanes(jnp.where(diag, jnp.broadcast_to(srow_ref[step], tile), 0))
         keep(step, key < POS, key, seg)
@@ -320,11 +330,6 @@
     facts = jnp.zeros((1, LANES), F32)
     for no, val in enumerate(first + last + [ones_where(cut > NEG)]):
         facts = jnp.where(lane_one == no, val, facts)
-
-    hot_low_ref[...] = hot(low_col == iota((1, plan.low_out), 1).astype(F32))
-    if more:
-        fold_ref[...] = unfold_hot(plan.low_out, plan.top_out)
-        hot_top_ref[...] = hot(top_col == iota((1, plan.top_out), 1).astype(F32))
 
     def apply(mask, recv, no):
         total = dot(mask[:, :plan.low], recv[:, :half])
@@ -406,15 +411,21 @@
             sums1[blk * big:(blk + 1) * big, half:] = dot(narrow, pile).astype(BF16)
     send_back(sums1, ret1, ret_sem1)
 
+    hot_low_ref[...] = hot(low_col == iota((1, plan.low_out), 1).astype(F32))
+    if more:
+        fold_ref[...] = unfold_hot(plan.low_out, plan.top_out)
+        hot_top_ref[...] = hot(top_col == iota((1, plan.top_out), 1).astype(F32))
+
     arrived(recv1.at[most], ret_sem0)
     if not more:
         for part in range(parts):
             start = part * cols
-            out_ref[:, start:start + half] = dot(hot_low_ref[...], ret0[part]).astype(BF16)
+            pay_ref[:, start:start + half] = dot(hot_low_ref[...], ret0[part]).astype(BF16)
     else:
         for part in range(parts):
             back_ref[:, part * half:(part + 1) * half] = dot(hot_low_ref[...], ret0[part])
     arrived(recv0.at[most], ret_sem1)
+    results = []
     if more:
         piles = jnp.concatenate([ret1[part, :, half:] for part in range(parts)], axis=1)
         piles = dot(fold_ref[...], piles).astype(BF16)
@@ -426,8 +437,15 @@
                                         for c in range(chunks)], axis=1)
             top_rows = dot(hot_top_ref[...], top_rows)
             rows = rows + top_rows[:, half:]
-            out_ref[:, start:start + half] = (back_ref[:, part * half:(part + 1) * half] + top_rows[:, :half]).astype(BF16)
-        out_ref[:, start + half:start + cols] = rows.astype(BF16)
+            pay_ref[:, start:start + half] = (back_ref[:, part * half:(part + 1) * half] + top_rows[:, :half]).astype(BF16)
+        pay_ref[:, start + half:start + cols] = rows.astype(BF16)
+        here = pl.ds(start, cols)
+        copy = pltpu.make_async_copy(pay_ref.at[:, here], out_hbm.at[:, here], out_sem.at[part])
+        copy.start()
+        results.append(copy)
+
+    for copy in results:
+        copy.wait()
 
     for like in (samp_all.at[rest], meta_all.at[rest], recv0.at[most], recv1.at[most], tails0, tails1, recv0.at[most],
                  recv1.at[most]):
@@ -472,20 +490,33 @@
         functools.partial(kernel, plan),
         out_shape=(jax.ShapeDtypeStruct((ROWS, WIDTH), BF16), jax.ShapeDtypeStruct((1, 1), F32)),
         in_specs=[vmem, vmem, pl.BlockSpec(memory_space=pl.ANY)],
-        out_specs=(vmem, pl.BlockSpec(memory_space=pltpu.SMEM)),
-        scratch_shapes=[pltpu.VMEM(*shape) for shape in shapes] + [pltpu.SemaphoreType.DMA] * 10,
+        out_specs=(pl.BlockSpec(memory_space=pl.ANY), pl.BlockSpec(memory_space=pltpu.SMEM)),
+        scratch_shapes=[pltpu.VMEM(*shape) for shape in shapes] + [pltpu.SemaphoreType.DMA] * 10
+        + [pltpu.SemaphoreType.DMA((plan.parts,))],
         compiler_params=pltpu.CompilerParams(collective_id=call_id, has_side_effects=True, vmem_limit_bytes=62 << 20),
     )(keys, segs, payload)
 
 
-def settle_kernel(src_ref, dst_ref):
-    dst_ref[...] = src_ref[...]
+def settle_kernel(src_ref, dst_ref, buf, in_sem, out_sem):
+    count = in_sem.shape[0]
+    tall = ROWS // count
+    rows = [pl.ds(no * tall, tall) for no in range(count)]
+    into = [pltpu.make_async_copy(src_ref.at[row], buf.at[row], in_sem.at[no]) for no, row in enumerate(rows)]
+    out = [pltpu.make_async_copy(buf.at[row], dst_ref.at[row], out_sem.at[no]) for no, row in enumerate(rows)]
+    for copy in into:
+        copy.start()
+    for no in range(count):
+        into[no].wait()
+        out[no].start()
+    for copy in out:
+        copy.wait()
 
 
 def settle(done):
-    block = pl.BlockSpec((ROWS // 4, WIDTH), lambda step: (step, 0))
-    return pl.pallas_call(settle_kernel, out_shape=jax.ShapeDtypeStruct((ROWS, WIDTH), BF16), grid=(4,),
-                          in_specs=[block], out_specs=block)(done)
+    here = pl.BlockSpec(memory_space=pl.ANY)
+    dma = pltpu.SemaphoreType.DMA((4,))
+    return pl.pallas_call(settle_kernel, out_shape=jax.ShapeDtypeStruct((ROWS, WIDTH), BF16), in_specs=[here],
+                          out_specs=here, scratch_shapes=[pltpu.VMEM((ROWS, WIDTH), BF16), dma, dma])(done)
 
 
 def solution(mesh):

time: 103 us -> 97.8 us (0.950); the launches traced: 101 us -> 97.6 us
  Pallas kernels: 100 us -> 96.9 us
    pallas_call x1, Pallas kernels: 96.7 us -> 94.5 us  [run(): pl.pallas_call(functools.partial(kernel, plan), out_shape=(jax.ShapeDtype...]
    pallas_call x1, Pallas kernels: 3.78 us -> 2.42 us  [settle(): pl.pallas_call(settle_kernel, out_shape=jax.ShapeDtypeStruct((ROWS, WIDTH...]
where the time goes in v5:
time: 97.8 us; the launch traced here: 97.6 us
  Pallas kernels  96.9 us (99%)
    pallas_call x1, Pallas kernels, run(): pl.pallas_call(functools.partial(kernel, plan), out_shape=(jax.ShapeDtype...  94.5 us
    pallas_call x1, Pallas kernels, settle(): pl.pallas_call(settle_kernel, out_shape=jax.ShapeDtypeStruct((ROWS, WIDTH...  2.42 us

profile of v5, /device:TPU:1, one launch (start us, length us, event | category | flops | bytes accessed | tf_op | source)
XLA Modules:
  0.0 97.6 jit_solution(2310357330112907246)
XLA Ops:
  0.0 0.0 copy-start.1
  0.0 0.0 copy-start
  0.0 94.5 %shard_map.37 = (bf16[512,2048]{1,0:T(8,128)(2,1)}, f32[1,1]{1,0:T(1,128)}) custom-call(f32[1,512]{1,0:T(1,128)} %bitcast.3, s32[1,512]{1,0:T(1,128)} %bitcast.5, bf16[512,2048]{1,0:T(8,128)(2,1)} %pay_hbm.1), custom_call_target="tpu_custom_call" | custom-call | tf_op jit(solution)/shard_map/pallas_call | solution.py:489
  95.0 0.0 copy-done.1
  95.0 0.0 copy-done
  95.1 2.4 %shard_map.38 = bf16[512,2048]{1,0:T(8,128)(2,1)} custom-call(bf16[512,2048]{1,0:T(8,128)(2,1)} %get-tuple-element.23.src_ref), custom_call_target="tpu_custom_call" | custom-call | tf_op jit(solution)/shard_map/pallas_call | solution.py:518
  (1 shorter events, 0.0 us)
Async XLA Ops:
  0.0 95.0 %copy-start.1 = (s32[512]{0:T(512)S(1)}, s32[512]{0:T(512)}, u32[]{:S(2)}) copy-start(s32[512]{0:T(512)} %param.6) | copy-start | bytes 6148
  0.0 95.0 %copy-start = (f32[512]{0:T(512)S(1)}, f32[512]{0:T(512)}, u32[]{:S(2)}) copy-start(f32[512]{0:T(512)} %param.5) | copy-start | bytes 6148

commit v6 on v5

--- a/solution.py
+++ b/solution.py
@@ -21,7 +21,7 @@
 BASE = 16
 MORE = 4
 FLAG = LANES - 1
-TALL = 128
+TALL = 256
 RING = 4
 
 
@@ -342,13 +342,13 @@
 
     big = 256
 
-    def products(recv, no):
+    def products(recv, no, first, last):
         def step(blk, carry):
             rows = pl.ds(pl.multiple_of(blk * big, big), big)
             acc_ref[rows] = apply(mask_ref[rows], recv, no)
             return carry
 
-        lax.fori_loop(0, plan.need // big, step, 0)
+        lax.fori_loop(first // big, last // big, step, 0)
 
     arrived(recv0.at[most], row_sem0)
     piled = big // quarters
@@ -361,7 +361,7 @@
     tail_msg0[:, :half] = apply(tail_hot, recv0, 0)[:1]
     tail_msg0[:, half:] = facts
     send_tail(tail_msg0, tail_all0, tail_sem0)
-    products(recv0, 0)
+    products(recv0, 0, 0, plan.low)
     arrived(recv1.at[most], row_sem1)
     tail_msg1[...] = apply(tail_hot, recv1, 1)[:1]
     send_tail(tail_msg1, tail_all1, tail_sem1)
@@ -378,33 +378,41 @@
     last_stop = jnp.max(jnp.where(stop, range_no, -1), axis=0, keepdims=True)
     linked = before & ((range_no > last_stop) | ((range_no == last_stop) & same_last))
 
-    def finish(tails, no, sums):
-        carry_in = along_sublanes(jnp.where(linked, tails[:, 0, :half], 0.0))
-
-        def closed(rows):
-            return (acc_ref[rows] + jnp.where(bcol_ref[rows][:, :1] == NEG, carry_in, 0.0)).astype(BF16)
+    def carried(tails):
+        return along_sublanes(jnp.where(linked, tails[:, 0, :half], 0.0))
+
+    def closed(rows, carry_in):
+        return (acc_ref[rows] + jnp.where(bcol_ref[rows][:, :1] == NEG, carry_in, 0.0)).astype(BF16)
+
+    def finish(tails, sums):
+        carry_in = carried(tails)
 
         def step(blk, carry):
             rows = pl.ds(pl.multiple_of(blk * big, big), big)
-            sums[rows, :half] = closed(rows)
+            sums[rows, :half] = closed(rows, carry_in)
             return carry
 
         lax.fori_loop(0, plan.low // big, step, 0)
-        if more:
-            top_done[:, no * half:(no + 1) * half] = closed(pl.ds(plan.low, plan.top))
 
     def send_back(src, dst, sem):
         for dev in others:
             remote(src.at[at16(dev)], dst.at[my_part, at16(my_range)], sem, dev).start()
         dst[my_part, at16(my_range)] = src[at16(me)]
 
-    finish(tail_all0, 0, sums0)
+    def finish_top(tails, no):
+        top_done[:, no * half:(no + 1) * half] = closed(pl.ds(plan.low, plan.top), carried(tails))
+
+    finish(tail_all0, sums0)
     send_back(sums0, ret0, ret_sem0)
 
-    products(recv1, 1)
+    if more:
+        products(recv0, 0, plan.low, plan.need)
+        finish_top(tail_all0, 0)
+    products(recv1, 1, 0, plan.need)
     arrived(tails1, tail_sem1)
-    finish(tail_all1, 1, sums1)
-    if more:
+    finish(tail_all1, sums1)
+    if more:
+        finish_top(tail_all1, 1)
         narrow = fold_hot(big, piled)
         for blk in range(plan.top // piled):
             pile = stack(top_done[blk * piled:(blk + 1) * piled], chunks)

time: 97.8 us -> 96.6 us (0.988)
  Pallas kernels: 96.9 us -> 95.7 us
    pallas_call x1, Pallas kernels: 94.5 us -> 93.2 us  [run(): pl.pallas_call(functools.partial(kernel, plan), out_shape=(jax.ShapeDtype...]
where the time goes in v6:
time: 96.6 us; the launch traced here: 96.4 us
  Pallas kernels  95.7 us (99%)
    pallas_call x1, Pallas kernels, run(): pl.pallas_call(functools.partial(kernel, plan), out_shape=(jax.ShapeDtype...  93.2 us
    pallas_call x1, Pallas kernels, settle(): pl.pallas_call(settle_kernel, out_shape=jax.ShapeDtypeStruct((ROWS, WIDTH...  2.42 us

profile of v6, /device:TPU:1, one launch (start us, length us, event | category | flops | bytes accessed | tf_op | source)
XLA Modules:
  0.0 96.4 jit_solution(14637220363638786268)
XLA Ops:
  0.0 0.0 copy-start.1
  0.0 0.0 copy-start
  0.0 93.2 %shard_map.37 = (bf16[512,2048]{1,0:T(8,128)(2,1)}, f32[1,1]{1,0:T(1,128)}) custom-call(f32[1,512]{1,0:T(1,128)} %bitcast.3, s32[1,512]{1,0:T(1,128)} %bitcast.5, bf16[512,2048]{1,0:T(8,128)(2,1)} %pay_hbm.1), custom_call_target="tpu_custom_call" | custom-call | tf_op jit(solution)/shard_map/pallas_call | solution.py:497
  93.8 0.0 copy-done.1
  93.8 0.0 copy-done
  93.8 2.4 %shard_map.38 = bf16[512,2048]{1,0:T(8,128)(2,1)} custom-call(bf16[512,2048]{1,0:T(8,128)(2,1)} %get-tuple-element.23.src_ref), custom_call_target="tpu_custom_call" | custom-call | tf_op jit(solution)/shard_map/pallas_call | solution.py:526
  (1 shorter events, 0.0 us)
Async XLA Ops:
  0.0 93.8 %copy-start.1 = (s32[512]{0:T(512)S(1)}, s32[512]{0:T(512)}, u32[]{:S(2)}) copy-start(s32[512]{0:T(512)} %param.6) | copy-start | bytes 6148
  0.0 93.8 %copy-start = (f32[512]{0:T(512)S(1)}, f32[512]{0:T(512)}, u32[]{:S(2)}) copy-start(f32[512]{0:T(512)} %param.5) | copy-start | bytes 6148

commit v7 on v6

--- a/solution.py
+++ b/solution.py
@@ -118,9 +118,9 @@
 
 def kernel(plan, keys_ref, segs_ref, pay_hbm, out_hbm, flag_ref, pay_ref, samp_msg, samp_all, fold_ref, packed0, packed1,
            recv0, recv1, meta_msg, meta_all, mask_ref, kcol_ref, scol_ref, bcol_ref, krow_ref, srow_ref, tail_msg0,
-           tail_msg1, tail_all0, tail_all1, top_ref, acc_ref, top_done, sums0, sums1, ret0, ret1, back_ref, hot_low_ref,
+           tail_msg1, tail_all0, tail_all1, top_ref, acc_ref, top_done, sums0, sums1, sums_top, ret0, ret1, ret_top, back_ref, hot_low_ref,
            hot_top_ref, pay_sem, send_sem, samp_sem, meta_sem, row_sem0, row_sem1, tail_sem0, tail_sem1, ret_sem0,
-           ret_sem1, out_sem):
+           ret_sem1, lines_sem, out_sem):
     parts, more, cols, half, chunks = plan.parts, plan.more, plan.cols, plan.half, plan.chunks
     me = lax.axis_index('group')
     my_range = me >> plan.shift
@@ -410,13 +410,14 @@
         finish_top(tail_all0, 0)
     products(recv1, 1, 0, plan.need)
     arrived(tails1, tail_sem1)
-    finish(tail_all1, sums1)
     if more:
         finish_top(tail_all1, 1)
         narrow = fold_hot(big, piled)
         for blk in range(plan.top // piled):
             pile = stack(top_done[blk * piled:(blk + 1) * piled], chunks)
-            sums1[blk * big:(blk + 1) * big, half:] = dot(narrow, pile).astype(BF16)
+            sums_top[blk * big:(blk + 1) * big] = dot(narrow, pile).astype(BF16)
+        send_back(sums_top, ret_top, lines_sem)
+    finish(tail_all1, sums1)
     send_back(sums1, ret1, ret_sem1)
 
     hot_low_ref[...] = hot(low_col == iota((1, plan.low_out), 1).astype(F32))
@@ -432,20 +433,25 @@
     else:
         for part in range(parts):
             back_ref[:, part * half:(part + 1) * half] = dot(hot_low_ref[...], ret0[part])
-    arrived(recv0.at[most], ret_sem1)
-    results = []
-    if more:
-        piles = jnp.concatenate([ret1[part, :, half:] for part in range(parts)], axis=1)
+    if more:
+        arrived(sums_top.at[most], lines_sem)
+        piles = jnp.concatenate([ret_top[part] for part in range(parts)], axis=1)
         piles = dot(fold_ref[...], piles).astype(BF16)
-    for part in range(parts):
-        start = part * cols
-        rows = dot(hot_low_ref[...], ret1[part, :, :half])
-        if more:
+        for part in range(parts):
+            start = part * cols
+            low = slice(part * half, (part + 1) * half)
             top_rows = jnp.concatenate([piles[c * plan.top_out:(c + 1) * plan.top_out, part * LANES:(part + 1) * LANES]
                                         for c in range(chunks)], axis=1)
             top_rows = dot(hot_top_ref[...], top_rows)
-            rows = rows + top_rows[:, half:]
-            pay_ref[:, start:start + half] = (back_ref[:, part * half:(part + 1) * half] + top_rows[:, :half]).astype(BF16)
+            pay_ref[:, start:start + half] = (back_ref[:, low] + top_rows[:, :half]).astype(BF16)
+            back_ref[:, low] = top_rows[:, half:]
+    arrived(recv1.at[most], ret_sem1)
+    results = []
+    for part in range(parts):
+        start = part * cols
+        rows = dot(hot_low_ref[...], ret1[part])
+        if more:
+            rows = rows + back_ref[:, part * half:(part + 1) * half]
         pay_ref[:, start + half:start + cols] = rows.astype(BF16)
         here = pl.ds(start, cols)
         copy = pltpu.make_async_copy(pay_ref.at[:, here], out_hbm.at[:, here], out_sem.at[part])
@@ -455,8 +461,8 @@
     for copy in results:
         copy.wait()
 
-    for like in (samp_all.at[rest], meta_all.at[rest], recv0.at[most], recv1.at[most], tails0, tails1, recv0.at[most],
-                 recv1.at[most]):
+    for like in (samp_all.at[rest], meta_all.at[rest], recv0.at[most], recv1.at[most], tails0, tails1, recv1.at[most],
+                 recv1.at[most]) + ((sums_top.at[most],) if more else ()):
         left(like)
 
 
@@ -487,9 +493,11 @@
         ((plan.need, plan.half), F32),
         ((max(plan.top, BASE), plan.cols), BF16),
         ((plan.low, plan.half), BF16),
-        ((plan.low, plan.long), BF16),
+        ((plan.low, plan.half), BF16),
+        ((plan.low if plan.more else BASE, LANES), BF16),
         ((plan.parts, plan.low_out, plan.half), BF16),
-        ((plan.parts, plan.low_out, plan.long), BF16),
+        ((plan.parts, plan.low_out, plan.half), BF16),
+        ((plan.parts, plan.low_out if plan.more else BASE, LANES), BF16),
         ((ROWS, WIDTH // 2) if plan.more else (8, LANES), F32),
         ((ROWS, plan.low_out), BF16),
         ((ROWS, max(plan.top_out, LANES)), BF16),
@@ -499,7 +507,7 @@
         out_shape=(jax.ShapeDtypeStruct((ROWS, WIDTH), BF16), jax.ShapeDtypeStruct((1, 1), F32)),
         in_specs=[vmem, vmem, pl.BlockSpec(memory_space=pl.ANY)],
         out_specs=(pl.BlockSpec(memory_space=pl.ANY), pl.BlockSpec(memory_space=pltpu.SMEM)),
-        scratch_shapes=[pltpu.VMEM(*shape) for shape in shapes] + [pltpu.SemaphoreType.DMA] * 10
+        scratch_shapes=[pltpu.VMEM(*shape) for shape in shapes] + [pltpu.SemaphoreType.DMA] * 11
         + [pltpu.SemaphoreType.DMA((plan.parts,))],
         compiler_params=pltpu.CompilerParams(collective_id=call_id, has_side_effects=True, vmem_limit_bytes=62 << 20),
     )(keys, segs, payload)

time: 96.6 us -> 95.3 us (0.987)
  Pallas kernels: 95.7 us -> 94.4 us
    pallas_call x1, Pallas kernels: 93.2 us -> 92 us  [run(): pl.pallas_call(functools.partial(kernel, plan), out_shape=(jax.ShapeDtype...]
where the time goes in v7:
time: 95.3 us; the launch traced here: 95.2 us
  Pallas kernels  94.4 us (99%)
    pallas_call x1, Pallas kernels, run(): pl.pallas_call(functools.partial(kernel, plan), out_shape=(jax.ShapeDtype...  92 us
    pallas_call x1, Pallas kernels, settle(): pl.pallas_call(settle_kernel, out_shape=jax.ShapeDtypeStruct((ROWS, WIDTH...  2.42 us

profile of v7, /device:TPU:1, one launch (start us, length us, event | category | flops | bytes accessed | tf_op | source)
XLA Modules:
  0.0 95.2 jit_solution(5582949671646231796)
XLA Ops:
  0.0 0.0 copy-start.1
  0.0 0.0 copy-start
  0.0 92.0 %shard_map.37 = (bf16[512,2048]{1,0:T(8,128)(2,1)}, f32[1,1]{1,0:T(1,128)}) custom-call(f32[1,512]{1,0:T(1,128)} %bitcast.3, s32[1,512]{1,0:T(1,128)} %bitcast.5, bf16[512,2048]{1,0:T(8,128)(2,1)} %pay_hbm.1), custom_call_target="tpu_custom_call" | custom-call | tf_op jit(solution)/shard_map/pallas_call | solution.py:505
  92.5 0.0 copy-done.1
  92.5 0.0 copy-done
  92.6 2.4 %shard_map.38 = bf16[512,2048]{1,0:T(8,128)(2,1)} custom-call(bf16[512,2048]{1,0:T(8,128)(2,1)} %get-tuple-element.23.src_ref), custom_call_target="tpu_custom_call" | custom-call | tf_op jit(solution)/shard_map/pallas_call | solution.py:534
  (1 shorter events, 0.0 us)
Async XLA Ops:
  0.0 92.5 %copy-start.1 = (s32[512]{0:T(512)S(1)}, s32[512]{0:T(512)}, u32[]{:S(2)}) copy-start(s32[512]{0:T(512)} %param.6) | copy-start | bytes 6148
  0.0 92.5 %copy-start = (f32[512]{0:T(512)S(1)}, f32[512]{0:T(512)}, u32[]{:S(2)}) copy-start(f32[512]{0:T(512)} %param.5) | copy-start | bytes 6148
